TPU v7x, 128 devices: a whole 4x4x4 slice. The times are simulated.
128 devices in a mesh: branch: 4 (over z_lo, core), shard: 32 (over y, x, z_hi).
Axes of the slice: x: 4, y: 4, z: 4 (z_hi: 2, z_lo: 2; z = z_hi * 2 + z_lo), core: 2. Of those that a mesh axis runs over, the one named last changes fastest.
Arguments:
- attention_weights: bfloat16 [4, 2, 4096, 4096], P('branch', None, None, 'shard'), may hold values from -1.25 to 1.25
- ffn_weights: bfloat16 [4, 3, 4096, 11008], P('branch', None, 'shard'), may hold values from -0.3125 to 0.3125
- tokens: bfloat16 [2048, 4096], P(('branch', 'shard')), may hold values from -6 to 6
- routes: int32 [2048, 2], P(('branch', 'shard')), may hold values from 0 to 3, all different within a row; in each aligned block of 16 rows (0 to 15, 16 to 31, ...) at most 12 rows name the same one
- router: bfloat16 [4096, 4], replicated, may hold values from -0.09375 to 0.09375
Outputs:
- merged_attention: bfloat16 [2, 4096, 4096], P(None, 'branch', 'shard')
- expert_weights: bfloat16 [4, 3, 4096, 11008], P('branch', None, None, 'shard')
- mixed_output: bfloat16 [2048, 4096], P(('branch', 'shard'))
Inputs may be any that keep to these rules, and one draw needn't show every extreme that they name: `routes`: the 2 experts of a row differ. In each aligned block of 16 rows (the rows of one device) no expert is named by more than 12 rows, and in some blocks one expert is named by exactly 12 rows.
All inputs are finite; a program needn't handle non-finite values.
Results may differ from a plain program's by a relative error of at most 0.018.
Values may be sent and summed in bfloat16 or wider, within the bound.
A program may use at most 192 MiB of HBM per device.

v0:
```python
import jax
import jax.numpy as jnp
from jax import lax
from jax.sharding import Mesh
from jax.sharding import PartitionSpec as P

SHARD = ("shard_0", "shard_1", "shard_2")
BRANCH_SHARD = ("branch", "shard_0", "shard_1", "shard_2")


def own_rows(terms, axes):
    running = terms.astype(jnp.bfloat16)
    for axis in axes:
        running = lax.psum_scatter(running, axis, scatter_dimension=0, tiled=True)
    return running.astype(jnp.float32)


def slot_table(route_rows, experts_count, capacity):
    chosen = (route_rows[:, :, None] == jnp.arange(experts_count, dtype=jnp.int32)).astype(
        jnp.int32
    )
    flat_picks = chosen.reshape(-1, experts_count)
    before = jnp.cumsum(flat_picks, axis=0) - flat_picks
    position = jnp.sum(before * flat_picks, axis=1)
    slot_id = route_rows.reshape(-1) * capacity + position
    one_hot = (slot_id[:, None] == jnp.arange(experts_count * capacity, dtype=jnp.int32)).astype(
        jnp.float32
    )
    return jnp.sum(one_hot.reshape(route_rows.shape[0], route_rows.shape[1], -1), axis=1)


def local(attention_weights, ffn_weights, tokens, routes, router):
    branches = lax.axis_size("branch")
    expert_weights = lax.all_to_all(ffn_weights, SHARD, split_axis=3, concat_axis=2, tiled=True)
    gate_weight = expert_weights[0, 0]
    up_weight = expert_weights[0, 1]
    down_weight = expert_weights[0, 2]
    tok_count = tokens.shape[0]
    model_width = tokens.shape[1]
    capacity = 3 * tok_count // 4
    slot_map = slot_table(routes, branches, capacity)
    buffers = lax.dot_general(
        slot_map.astype(jnp.bfloat16),
        tokens,
        (((0,), (0,)), ((), ())),
        preferred_element_type=jnp.float32,
    )
    buffers = buffers.astype(jnp.bfloat16).reshape(branches, capacity, model_width)
    arrived = lax.all_to_all(buffers, "branch", split_axis=0, concat_axis=0, tiled=True)
    slot_rows = lax.all_gather(
        arrived.reshape(branches * capacity, model_width), SHARD, axis=0, tiled=True
    )
    gate_proj = jnp.dot(slot_rows, gate_weight, preferred_element_type=jnp.float32)
    up_proj = jnp.dot(slot_rows, up_weight, preferred_element_type=jnp.float32)
    hidden = (jax.nn.silu(gate_proj) * up_proj).astype(jnp.bfloat16)
    summed = own_rows(
        lax.dot_general(
            hidden, down_weight, (((1,), (1,)), ((), ())), preferred_element_type=jnp.float32
        ),
        SHARD,
    )
    outputs = summed.astype(jnp.bfloat16).reshape(branches, capacity, model_width)
    returned = lax.all_to_all(outputs, "branch", split_axis=0, concat_axis=0, tiled=True)
    gates_all = jax.nn.sigmoid(jnp.dot(tokens, router, preferred_element_type=jnp.float32))
    weighting = slot_map * jnp.repeat(gates_all, capacity, axis=1)
    mixed_output = jnp.dot(
        weighting, returned.reshape(branches * capacity, model_width).astype(jnp.float32)
    )
    mixed_output = mixed_output.astype(jnp.bfloat16)
    traded = lax.all_to_all(attention_weights, "branch", split_axis=2, concat_axis=0, tiled=True)
    summed_attention = jnp.sum(traded.astype(jnp.float32), axis=0)
    merged_attention = (summed_attention * (1.0 / branches)).astype(jnp.bfloat16)
    return (merged_attention, expert_weights, mixed_output)


def solution(mesh):
    torus = Mesh(
        mesh.devices.reshape(mesh.shape["branch"], 4, 4, 2),
        ("branch", "shard_0", "shard_1", "shard_2"),
    )
    in_specs = (
        P("branch", None, None, SHARD),
        P("branch", None, SHARD, None),
        P(BRANCH_SHARD, None),
        P(BRANCH_SHARD, None),
        P(),
    )
    out_specs = (P(None, "branch", SHARD), P("branch", None, None, SHARD), P(BRANCH_SHARD, None))
    return jax.shard_map(local, mesh=torus, in_specs=in_specs, out_specs=out_specs, check_vma=False)
```

profile of v0, /device:TPU:0, one launch (start us, length us, event | category | flops | bytes accessed | tf_op | source)
XLA Modules:
  0.0 517.8 jit_solution(2717877055317344785)
XLA Ops:
  7.2 0.0 copy-start
  7.2 0.0 all-gather.2.cloned.1.call-start
  7.2 0.8 copy.58
  8.0 0.1 eq.30
  8.1 0.1 fusion.13
  8.2 0.1 reduce_window_sum.11
  8.2 0.2 select_reduce_fusion
  8.4 0.1 reduce_sum.33
  8.5 0.1 copy.59
  8.6 0.7 multiply_add_fusion
  9.3 0.1 convert_reduce_fusion.1
  9.4 0.0 copy-done
  9.4 0.3 convolution_convert_fusion.1
  9.7 0.1 reshape.45
  9.8 11.9 %all_to_all.37 = bf16[4,12,4096]{2,1,0:T(8,128)(2,1)S(1)} all-to-all(bf16[4,12,4096]{2,1,0:T(8,128)(2,1)S(1)} %reshape.45), channel_id=1, replica_groups=mesh['branch'=4,'shard_0'=4,'shard_1'=4,'shard_2'=2] {'branch'}, dimensions={0} | all-to-all | bytes 786432 | tf_op jit(solution)/shard_map/all_to_all | solution.py:49
  21.7 0.8 reshape.46
  22.5 0.0 all-gather.2.cloned.1.call-update
  22.5 0.0 reduce-scatter.4.cloned.1.call-start
  22.6 17.5 %copy.55 = bf16[1,3,128,11008]{2,1,0,3:T(4,128)(2,1)} copy(bf16[1,3,128,11008]{3,2,1,0:T(8,128)(2,1)} %param.6) | data formatting | bytes 16908288 | tf_op args[1]
  40.1 147.4 %all_to_all.38 = bf16[1,3,128,11008]{2,1,0,3:T(4,128)(2,1)S(1)} all-to-all(bf16[1,3,128,11008]{2,1,0,3:T(4,128)(2,1)} %copy.55), channel_id=1, replica_groups=mesh['branch'=4,'shard_0'=4,'shard_1'=4,'shard_2'=2] {'shard_0','shard_1..., dimensions={3} | all-to-all | bytes 16908288 | tf_op jit(solution)/shard_map/all_to_all | solution.py:34
  187.5 5.0 copy.56
  192.6 9.5 %copy.67 = bf16[1,3,32,43,8,128]{5,4,2,3,1,0:T(8,128)(2,1)} copy(bf16[1,3,32,43,8,128]{5,4,3,2,1,0:T(8,128)(2,1)} %bitcast.32) | data formatting | bytes 16908288 | tf_op jit(solution)/shard_map/all_to_all | solution.py:34
  202.1 65.7 %all-gather.2.cloned.1.call-done = bf16[1536,4096]{1,0:T(8,128)(2,1)} async-done(((bf16[48,4096]{1,0:T(8,128)(2,1)}), bf16[1536,4096]{1,0:T(8,128)(2,1)}) %all-gather.2.cloned.1.call-update) | async-done | bytes 12582928 | tf_op jit(solution)/shard_map/all_gather | solution.py:50
  267.7 8.5 %fusion.1 = f32[1536,344]{0,1:T(8,128)S(1)} fusion(bf16[1536,4096]{1,0:T(8,128)(2,1)} %all-gather.2.cloned.1.call-done, bf16[1,3,4096,344]{2,3,1,0:T(8,128)(2,1)} %bitcast.33), kind=kOutput, calls=%fused_computation.10 | convolution fusion | flops 4328521728 | bytes 17514496 | tf_op jit(solution)/shard_map/dot_general | solution.py:53
  276.2 21.6 %convolution_convert_fusion = bf16[1536,4096]{1,0:T(8,128)(2,1)} fusion(bf16[1,3,4096,344]{2,3,1,0:T(8,128)(2,1)} %bitcast.34, bf16[1536,4096]{1,0:T(8,128)(2,1)} %all-gather.2.cloned.1.call-done, f32[1536,344]{0,1:T(8,128)S(1)} %fusion.1), kind=kOutput, calls=%fused_computation | convolution fusion | flops 8666505216 | bytes 32915456 | tf_op jit(solution)/shard_map/dot_general | solution.py:57
  297.7 0.0 reduce-scatter.4.cloned.1.call-update
  297.8 0.0 copy-start.1
  297.8 0.0 reduce-scatter.6.cloned.1.call-start
  297.8 112.3 %reduce-scatter.4.cloned.1.call-done = bf16[384,4096]{1,0:T(8,128)(2,1)} async-done(((bf16[1536,4096]{1,0:T(8,128)(2,1)}), bf16[384,4096]{1,0:T(8,128)(2,1)}) %reduce-scatter.4.cloned.1.call-update) | async-done | bytes 3145744 | tf_op jit(solution)/shard_map/reduce_scatter | solution.py:14
  410.1 0.0 reduce-scatter.6.cloned.1.call-update
  410.1 0.2 reduce-scatter.8.cloned.1.call-start
  410.4 40.1 %reduce-scatter.6.cloned.1.call-done = bf16[96,4096]{1,0:T(8,128)(2,1)} async-done(((bf16[384,4096]{1,0:T(8,128)(2,1)}), bf16[96,4096]{1,0:T(8,128)(2,1)}) %reduce-scatter.6.cloned.1.call-update) | async-done | bytes 786448 | tf_op jit(solution)/shard_map/reduce_scatter | solution.py:14
  450.5 0.0 reduce-scatter.8.cloned.1.call-update
  450.5 18.1 %copy.54 = bf16[1,2,4096,128]{3,1,0,2:T(2,128)(2,1)} copy(bf16[1,2,4096,128]{3,2,1,0:T(8,128)(2,1)S(1)} %copy-done.1) | data formatting | bytes 4194304 | tf_op args[0]
  468.7 3.7 all-to-all-start
  472.4 0.1 reduce_sum.35
  472.5 0.2 fusion.10
  472.7 0.1 copy.60
  472.8 0.1 broadcast_multiply_fusion
  472.9 1.3 reduce-scatter.8.cloned.1.call-done
  474.2 1.9 reshape.47
  476.1 22.0 %all-to-all-done = bf16[1,2,4096,128]{3,1,0,2:T(2,128)(2,1)S(1)} async-done(((bf16[1,2,4096,128]{3,1,0,2:T(2,128)(2,1)}), bf16[1,2,4096,128]{3,1,0,2:T(2,128)(2,1)S(1)}, u32[]{:S(2)}, u32[]{:S(2)}) %all-to-all-start) | async-done | bytes 2097184 | tf_op jit(solution)/shard_map/all_to_all | solution.py:70
  498.1 3.5 all-to-all-start.3
  501.5 2.1 convert_reduce_fusion
  503.6 0.5 multiply_convert_fusion
  504.1 0.9 copy.62
  505.0 5.3 %all-to-all-done.3 = bf16[4,12,4096]{2,1,0:T(8,128)(2,1)S(1)} async-done(((bf16[4,12,4096]{2,1,0:T(8,128)(2,1)}), bf16[4,12,4096]{2,1,0:T(8,128)(2,1)S(1)}, u32[]{:S(2)}, u32[]{:S(2)}) %all-to-all-start.3) | async-done | bytes 393248 | tf_op jit(solution)/shard_map/all_to_all | solution.py:63
  510.3 1.0 fusion
  (3 shorter events, 0.0 us)
Async XLA Ops:
  7.2 2.2 copy-start
  7.2 260.5 %all-gather.2.cloned.1.call-start = ((), (), s32[]{:S(2)}) async-start(), calls=%async_computation.7 | async-start | bytes 12976128 | tf_op jit(solution)/shard_map/all_gather | solution.py:50
  22.5 387.6 %reduce-scatter.4.cloned.1.call-start = ((), (), s32[]{:S(2)}) async-start(), calls=%async_computation.8 | async-start | bytes 15728640 | tf_op jit(solution)/shard_map/reduce_scatter | solution.py:14
  297.8 152.8 %copy-start.1 = (bf16[1,2,4096,128]{3,2,1,0:T(8,128)(2,1)S(1)}, bf16[1,2,4096,128]{3,2,1,0:T(8,128)(2,1)}, u32[]{:S(2)}) copy-start(bf16[1,2,4096,128]{3,2,1,0:T(8,128)(2,1)} %param.5) | copy-start | bytes 6291460
  297.8 152.7 %reduce-scatter.6.cloned.1.call-start = ((), (), s32[]{:S(2)}) async-start(), calls=%async_computation.9 | async-start | bytes 3932160 | tf_op jit(solution)/shard_map/reduce_scatter | solution.py:14
  410.1 64.1 %reduce-scatter.8.cloned.1.call-start = ((), (), s32[]{:S(2)}) async-start(), calls=%async_computation.10 | async-start | bytes 1179648 | tf_op jit(solution)/shard_map/reduce_scatter | solution.py:14
  468.7 3.8 copy-start.2
  468.7 29.4 %all-to-all-start = ((bf16[1,2,4096,128]{3,1,0,2:T(2,128)(2,1)}), bf16[1,2,4096,128]{3,1,0,2:T(2,128)(2,1)S(1)}, u32[]{:S(2)}, u32[]{:S(2)}) async-start(bf16[1,2,4096,128]{3,1,0,2:T(2,128)(2,1)} %copy.54), calls=%async_computation | async-start | bytes 4194304 | tf_op jit(solution)/shard_map/all_to_all | solution.py:70
  498.1 12.3 %all-to-all-start.3 = ((bf16[4,12,4096]{2,1,0:T(8,128)(2,1)}), bf16[4,12,4096]{2,1,0:T(8,128)(2,1)S(1)}, u32[]{:S(2)}, u32[]{:S(2)}) async-start(bf16[4,12,4096]{2,1,0:T(8,128)(2,1)} %reshape.47), calls=%async_computation.6 | async-start | bytes 1048576 | tf_op jit(solution)/shard_map/all_to_all | solution.py:63
Sparse Core Ops, SparseCore 0:
  22.6 245.0 all-gather.1
  297.9 112.1 reduce-scatter.3
  412.5 37.9 reduce-scatter.5
  452.7 21.4 reduce-scatter.7
where the time goes:
time: 519 us; the launch traced here: 518 us
  waiting for transfers between devices  247 us (48%)
  blocking collectives  159 us (31%)
  local copies, waits for them, and re-layouts  55.1 us (11%)
  matrix products  31.4 us (6%)
  between operations  13.9 us (3%)
  starting transfers between devices  7.55 us (1%)
    reduce_scatter x3, waiting for transfers between devices, own_rows(): running = lax.psum_scatter(running, axis, scatter_dimension=0, tiled=True)  154 us
    all_to_all x1, blocking collectives, local(): lax.all_to_all(ffn_weights, SHARD, split_axis=3, concat_axis=2, tiled=True)  147 us
    all_gather x1, waiting for transfers between devices, local(): lax.all_gather(arrived.reshape(branches * capacity, model_width), SHARD,...  65.7 us
    unnamed x10, local copies, waits for them, and re-layouts  37.3 us
    all_to_all x1, waiting for transfers between devices, local(): lax.all_to_all(attention_weights, 'branch', split_axis=2, concat_axis=0,...  22 us
    dot_general x1, matrix products, local(): lax.dot_general(hidden, down_weight, (((1,), (1,)), ((), ())), preferred_...  21.6 us
    all_to_all x2, local copies, waits for them, and re-layouts, local(): lax.all_to_all(ffn_weights, SHARD, split_axis=3, concat_axis=2, tiled=True)  14.5 us
    all_to_all x1, blocking collectives, local(): lax.all_to_all(buffers, 'branch', split_axis=0, concat_axis=0, tiled=True)  11.9 us
  transfers between devices with their start and end apart: 6, of which 6 were waited for; matrix products, arithmetic and copies ran while one was open for 11% of the time, Pallas kernels for 0%

commit v1 on v0

v1 whole, which is shorter than its diff:
```python
import jax
import jax.numpy as jnp
from jax import lax
from jax.experimental import pallas as pl
from jax.experimental.pallas import tpu as pltpu
from jax.sharding import Mesh
from jax.sharding import PartitionSpec as P

MESH = pl.DeviceIdType.MESH
BF16 = jnp.bfloat16
F32 = jnp.float32

ROUNDS = []
for _a in (0, 1):
    ROUNDS += [
        [(1, 1, _a), (3, 3, 1 - _a)],
        [(1, 3, _a), (3, 1, 1 - _a)],
        [(1, 2, _a), (3, 0, 1 - _a)],
        [(3, 2, _a), (1, 0, 1 - _a)],
        [(2, 1, _a), (0, 3, 1 - _a)],
        [(2, 3, _a), (0, 1, 1 - _a)],
    ]
ROUNDS += [[(2, 2, 1)], [(2, 2, 0), (0, 0, 1)], [(2, 0, 1), (0, 2, 0)], [(2, 0, 0), (0, 2, 1)]]
ORDERS = (("x", "y", "z"), ("y", "z", "x"), ("z", "x", "y"))
WINDOW = 2


class Place:
    def __init__(self):
        self.y, self.x = lax.axis_index("y"), lax.axis_index("x")
        self.zh, self.zl = lax.axis_index("zh"), lax.axis_index("zl")
        self.core = lax.axis_index("core")
        self.z = self.zh * 2 + self.zl
        self.at = {"x": self.x, "y": self.y, "z": self.z}

    def shift(self, axis, k):
        return lax.rem(self.at[axis] + k, 4)

    def along(self, axis, k):
        v = self.shift(axis, k)
        if axis == "z":
            return {"zh": v // 2, "zl": lax.rem(v, 2)}
        return {axis: v}

    def shard(self, o):
        return lax.rem(self.y + o[0], 4), lax.rem(self.x + o[1], 4), lax.rem(self.zh + o[2], 2)


def block_index(place, order, phase, coords=None):
    done = order[:phase]
    out = []
    for axis in ("z", "y", "x"):
        if axis in done:
            out.append(slice(None))
        else:
            out.append(place.at[axis] if coords is None or axis not in coords else coords[axis])
    return tuple(out)


def gather_kernel(wt, tok, att, ew, tall, arecv, wbuf, tbuf, abuf, ws, wr, gs, gr, cs, cr, as_, ar, ls):
    p = Place()
    me = (p.y * 4 + p.x) * 2 + p.zh
    branch = p.zl * 2 + p.core
    units, width = ew.shape[1], wt.shape[2]
    rows = att.shape[1] // 4
    third = tok.shape[1] // 3

    bar = pltpu.get_barrier_semaphore()
    peers = []
    for r in ROUNDS:
        for o in r:
            a, b, c = p.shard(o)
            peers.append({"y": a, "x": b, "zh": c})
    peers += [p.along("z", 1), p.along("z", 3)]
    peers += [{"core": 1 - p.core}, {"zl": 1 - p.zl, "core": 1 - p.core}]
    for q in peers:
        pl.semaphore_signal(bar, inc=1, device_id=q, device_id_type=MESH)
    pl.semaphore_wait(bar, len(peers))

    def lanes(c):
        return pl.ds(c * third, third)

    def gather_copies(phase):
        out = []
        for c, order in enumerate(ORDERS):
            src_at = block_index(p, order, phase) + (p.core, slice(None), lanes(c))
            dst = tall.at[src_at]
            src = tok.at[:, lanes(c)] if phase == 0 else dst
            for k in (1, 3, 2):
                i = (phase * 3 + c) * 3 + k - 1
                out.append(
                    pltpu.make_async_remote_copy(
                        src, dst, gs.at[i], gr.at[i],
                        device_id=p.along(order[phase], k), device_id_type=MESH,
                    )
                )
        return out

    def weight_copies(number, r):
        out = []
        for j, o in enumerate(r):
            a, b, c = p.shard(o)
            d = (a * 4 + b) * 2 + c
            i = number * 2 + j
            out.append(
                pltpu.make_async_remote_copy(
                    wt.at[:, pl.ds(pl.multiple_of(d * units, 8), units), :],
                    ew.at[:, :, pl.ds(pl.multiple_of(me * width, 128), width)],
                    ws.at[i], wr.at[i],
                    device_id={"y": a, "x": b, "zh": c}, device_id_type=MESH,
                )
            )
        return out

    def att_copies():
        out = []
        for j, (dz, dc) in enumerate(((1, 0), (1, 1), (0, 1))):
            z2 = lax.rem(p.zl + dz, 2)
            c2 = lax.rem(p.core + dc, 2)
            b2 = z2 * 2 + c2
            out.append(
                pltpu.make_async_remote_copy(
                    att.at[:, pl.ds(pl.multiple_of(b2 * rows, 8), rows), :],
                    arecv.at[j], as_.at[j], ar.at[j],
                    device_id={"zl": z2, "core": c2}, device_id_type=MESH,
                )
            )
        return out

    def start(copies):
        for cp in copies:
            cp.start()

    phases = [gather_copies(ph) for ph in range(3)]
    rounds = [weight_copies(n, r) for n, r in enumerate(ROUNDS)]
    start(phases[0])
    start(rounds[0])
    start(rounds[1])

    own = [
        (wt.at[:, pl.ds(pl.multiple_of(me * units, 8), units), :], wbuf,
         ew.at[:, :, pl.ds(pl.multiple_of(me * width, 128), width)]),
        (tok, tbuf, tall.at[p.z, p.y, p.x, p.core]),
        (att.at[:, pl.ds(pl.multiple_of(branch * rows, 8), rows), :], abuf, arecv.at[3]),
    ]
    ins = [pltpu.make_async_copy(s, v, ls.at[i]) for i, (s, v, _) in enumerate(own)]
    outs = [pltpu.make_async_copy(v, d, ls.at[3 + i]) for i, (_, v, d) in enumerate(own)]
    start(ins)
    for i in range(3):
        ins[i].wait()
        outs[i].start()
    for cp in outs:
        cp.wait()

    swap = [
        pltpu.make_async_remote_copy(
            tall.at[:, :, :, p.core, :, lanes(c)], tall.at[:, :, :, p.core, :, lanes(c)],
            cs.at[c], cr.at[c], device_id={"core": 1 - p.core}, device_id_type=MESH,
        )
        for c in range(3)
    ]
    acopies = att_copies()

    for cp in phases[0]:
        cp.wait()
    start(phases[1])
    for n in range(2, len(rounds)):
        for cp in rounds[n - WINDOW]:
            cp.wait_send()
        start(rounds[n])
        if n == 4:
            for cp in phases[1]:
                cp.wait()
            start(phases[2])
        if n == 12:
            for cp in phases[2]:
                cp.wait()
            start(swap)
            start(acopies)
    for n in range(len(rounds) - WINDOW, len(rounds)):
        for cp in rounds[n]:
            cp.wait_send()
    for r in rounds:
        for cp in r:
            cp.wait_recv()
    for cp in swap + acopies:
        cp.wait()


def gather(wt, tok, att):
    units = wt.shape[1] // 32
    rows = att.shape[1] // 4
    dma = pltpu.SemaphoreType.DMA
    return pl.pallas_call(
        gather_kernel,
        out_shape=(
            jax.ShapeDtypeStruct((3, units, wt.shape[2] * 32), BF16),
            jax.ShapeDtypeStruct((4, 4, 4, 2) + tok.shape, BF16),
            jax.ShapeDtypeStruct((4, 2, rows, att.shape[2]), BF16),
        ),
        in_specs=[pl.BlockSpec(memory_space=pl.ANY)] * 3,
        out_specs=[pl.BlockSpec(memory_space=pl.ANY)] * 3,
        scratch_shapes=[
            pltpu.VMEM((3, units, wt.shape[2]), BF16),
            pltpu.VMEM(tok.shape, BF16),
            pltpu.VMEM((2, rows, att.shape[2]), BF16),
            dma((32,)), dma((32,)), dma((27,)), dma((27,)), dma((3,)), dma((3,)), dma((3,)), dma((3,)),
            dma((6,)),
        ],
        compiler_params=pltpu.CompilerParams(collective_id=0, has_side_effects=True),
    )(wt, tok, att)


def colour_lanes(width):
    tiles = width // 128
    cut = [0, -(-tiles // 3), -(-tiles // 3) + (tiles - tiles // 3) // 2, tiles]
    return [(cut[i] * 128, (cut[i + 1] - cut[i]) * 128) for i in range(3)]


def scatter_kernel(part, out, own, r0, s0, r1, s1, r2, s2, r3, ss, rs, ls):
    p = Place()
    bar = pltpu.get_barrier_semaphore()
    peers = [{"core": 1 - p.core}] + [p.along(a, k) for a in ("x", "y", "z") for k in (1, 2, 3)]
    for q in peers:
        pl.semaphore_signal(bar, inc=1, device_id=q, device_id_type=MESH)
    pl.semaphore_wait(bar, len(peers))
    cuts = colour_lanes(part.shape[5])

    swaps, loads = [], []
    for c, (lo, n) in enumerate(cuts):
        swaps.append(
            pltpu.make_async_remote_copy(
                part.at[:, :, :, 1 - p.core, :, pl.ds(lo, n)], r0[c],
                ss.at[c], rs.at[c], device_id={"core": 1 - p.core}, device_id_type=MESH,
            )
        )
        loads.append(
            pltpu.make_async_copy(part.at[:, :, :, p.core, :, pl.ds(lo, n)], own[c], ls.at[c])
        )
    for a, b in zip(swaps, loads):
        a.start()
        b.start()

    stage1, stage2, stage3 = [], [], []

    def send(stage, c, axis, src_of, dst):
        copies = []
        for k in (1, 3, 2):
            i = 3 + (stage * 3 + c) * 3 + k - 1
            cp = pltpu.make_async_remote_copy(
                src_of(p.shift(axis, k)), dst.at[k - 1], ss.at[i], rs.at[i],
                device_id=p.along(axis, k), device_id_type=MESH,
            )
            cp.start()
            copies.append(cp)
        return copies

    def pick(ref, left, axis, v):
        return ref.at[tuple(v if a == axis else slice(None) for a in left)]

    def left_after(order, phase):
        return [a for a in ("z", "y", "x") if a not in order[:phase]]

    for c, order in enumerate(ORDERS):
        swaps[c].wait()
        loads[c].wait()

        def add(i, carry, c=c):
            at = (i // 16, lax.rem(i // 4, 4), lax.rem(i, 4))
            s0[c][at] = (own[c][at].astype(F32) + r0[c][at].astype(F32)).astype(BF16)
            return carry

        lax.fori_loop(0, 64, add, 0)
        left = left_after(order, 0)
        stage1.append(send(0, c, order[0], lambda v, c=c, left=left, a=order[0]: pick(s0[c], left, a, v), r1[c]))

    for c, order in enumerate(ORDERS):
        for cp in stage1[c]:
            cp.wait()
        mine = pick(s0[c], left_after(order, 0), order[0], p.at[order[0]])

        def add(i, carry, c=c, mine=mine):
            at = (i // 4, lax.rem(i, 4))
            total = mine[at].astype(F32)
            for k in range(3):
                total += r1[c][(k,) + at].astype(F32)
            s1[c][at] = total.astype(BF16)
            return carry

        lax.fori_loop(0, 16, add, 0)
        left = left_after(order, 1)
        stage2.append(send(1, c, order[1], lambda v, c=c, left=left, a=order[1]: pick(s1[c], left, a, v), r2[c]))

    for c, order in enumerate(ORDERS):
        for cp in stage2[c]:
            cp.wait()
        mine = pick(s1[c], left_after(order, 1), order[1], p.at[order[1]])

        def add(i, carry, c=c, mine=mine):
            total = mine[i].astype(F32)
            for k in range(3):
                total += r2[c][k, i].astype(F32)
            s2[c][i] = total.astype(BF16)
            return carry

        lax.fori_loop(0, 4, add, 0)
        left = left_after(order, 2)
        stage3.append(send(2, c, order[2], lambda v, c=c, left=left, a=order[2]: pick(s2[c], left, a, v), r3[c]))

    for c, order in enumerate(ORDERS):
        for cp in stage3[c]:
            cp.wait()
        total = s2[c][p.at[order[2]]].astype(F32)
        for k in range(3):
            total += r3[c][k].astype(F32)
        lo, n = cuts[c]
        out[:, lo:lo + n] = total.astype(BF16)


def scatter(part):
    rows, width = part.shape[4:]
    cuts = colour_lanes(width)
    dma = pltpu.SemaphoreType.DMA

    def bufs(*lead):
        return [pltpu.VMEM(lead + (rows, n), BF16) for _, n in cuts]

    return pl.pallas_call(
        scatter_kernel,
        out_shape=jax.ShapeDtypeStruct((rows, width), BF16),
        in_specs=[pl.BlockSpec(memory_space=pl.ANY)],
        out_specs=pl.BlockSpec(memory_space=pltpu.VMEM),
        scratch_shapes=[
            bufs(4, 4, 4), bufs(4, 4, 4), bufs(4, 4, 4),
            bufs(3, 4, 4), bufs(4, 4), bufs(3, 4), bufs(4), bufs(3),
            dma((30,)), dma((30,)), dma((3,)),
        ],
        compiler_params=pltpu.CompilerParams(
            collective_id=1, has_side_effects=True, vmem_limit_bytes=56 * 1024 * 1024
        ),
    )(part)


def local(attention_weights, ffn_weights, tokens, routes, router):
    experts = router.shape[1]
    width = tokens.shape[1]
    wt = jnp.swapaxes(ffn_weights[0], 1, 2)
    gates = jax.nn.sigmoid(jnp.dot(tokens, router, preferred_element_type=F32))
    named = jnp.sum((routes[:, :, None] == jnp.arange(experts, dtype=jnp.int32)).astype(F32), axis=1)
    weighting = named * gates
    high = lax.reduce_precision(weighting, 8, 7)
    low = (weighting - high).astype(BF16)
    high = high.astype(BF16)
    tok = jnp.concatenate(
        [tokens, high, low, jnp.zeros((tokens.shape[0], 128 - 2 * experts), BF16)], axis=1
    )
    ew, tall, arecv = gather(wt, tok, attention_weights[0])
    flat = tall.reshape(-1, tok.shape[1])
    rows = flat[:, :width]
    expert = lax.axis_index("zl") * 2 + lax.axis_index("core")
    pair = lax.dynamic_slice_in_dim(flat[:, width:width + experts], expert, 1, 1).astype(F32)
    pair += lax.dynamic_slice_in_dim(flat[:, width + experts:width + 2 * experts], expert, 1, 1).astype(F32)
    nt = (((1,), (1,)), ((), ()))
    gate_proj = lax.dot_general(rows, ew[0], nt, preferred_element_type=F32)
    up_proj = lax.dot_general(rows, ew[1], nt, preferred_element_type=F32)
    hidden = (jax.nn.silu(gate_proj) * up_proj * pair).astype(BF16)
    part = jnp.dot(hidden, ew[2], preferred_element_type=F32).astype(BF16)
    mixed_output = scatter(part.reshape(tall.shape[:5] + (width,)))
    merged = (jnp.sum(arecv.astype(F32), axis=0) * 0.25).astype(BF16)
    return merged, jnp.swapaxes(ew, 1, 2)[None], mixed_output


def solution(mesh):
    torus = Mesh(mesh.devices.reshape(2, 2, 4, 4, 2), ("zl", "core", "y", "x", "zh"))
    shard = ("y", "x", "zh")
    branch = ("zl", "core")
    in_specs = (
        P(branch, None, None, shard),
        P(branch, None, shard, None),
        P(branch + shard, None),
        P(branch + shard, None),
        P(),
    )
    out_specs = (P(None, branch, shard), P(branch, None, None, shard), P(branch + shard, None))
    return jax.shard_map(local, mesh=torus, in_specs=in_specs, out_specs=out_specs, check_vma=False)
```

time: 519 us -> 315 us (0.61)
  Pallas kernels: 0 us -> 252 us
  waiting for transfers between devices: 247 us -> 0 us
  blocking collectives: 159 us -> 0 us
  local copies, waits for them, and re-layouts: 55.1 us -> 24.6 us
  between operations: 13.9 us -> 0.72 us
  starting transfers between devices: 7.55 us -> 0 us
    pallas_call x0 -> x2, Pallas kernels: none -> 252 us  [the longest x1 176 us: gather(): pl.pallas_call(gather_kernel, out_shape=(jax.ShapeDtypeStruct((3, units,...]
    all_to_all x2 -> x0, blocking collectives: 159 us -> none  [the longest x1 147 us: local(): lax.all_to_all(ffn_weights, SHARD, split_axis=3, concat_axis=2, tiled=True)]
    reduce_scatter x3 -> x0, waiting for transfers between devices: 154 us -> none  [own_rows(): running = lax.psum_scatter(running, axis, scatter_dimension=0, tiled=True)]
    all_gather x1 -> x0, waiting for transfers between devices: 65.7 us -> none  [local(): lax.all_gather(arrived.reshape(branches * capacity, model_width), SHARD,...]
    all_to_all x2 -> x0, waiting for transfers between devices: 27.3 us -> none  [the longest x1 22 us: local(): lax.all_to_all(attention_weights, 'branch', split_axis=2, concat_axis=0,...]
    unnamed x10 -> x11, local copies, waits for them, and re-layouts: 37.3 us -> 21.1 us
    all_to_all x2 -> x0, local copies, waits for them, and re-layouts: 14.5 us -> none  [local(): lax.all_to_all(ffn_weights, SHARD, split_axis=3, concat_axis=2, tiled=True)]
    all_to_all x2 -> x0, starting transfers between devices: 7.21 us -> none  [the longest x1 3.74 us: local(): lax.all_to_all(attention_weights, 'branch', split_axis=2, concat_axis=0,...]
  transfers between devices with their start and end apart: 6 -> 0, of which waited for: 6 -> 0; matrix products, arithmetic and copies ran while one was open for 11% -> 0% of each run, Pallas kernels for 0% -> 0%
where the time goes in v1:
time: 315 us; the launch traced here: 314 us
  Pallas kernels  252 us (80%)
  matrix products  33.6 us (11%)
  local copies, waits for them, and re-layouts  24.6 us (8%)
  other arithmetic  3.63 us (1%)
    pallas_call x1, Pallas kernels, gather(): pl.pallas_call(gather_kernel, out_shape=(jax.ShapeDtypeStruct((3, units,...  176 us
    pallas_call x1, Pallas kernels, scatter(): pl.pallas_call(scatter_kernel, out_shape=jax.ShapeDtypeStruct((rows, widt...  75.8 us
    dot_general x1, matrix products, local(): part = jnp.dot(hidden, ew[2], preferred_element_type=F32).astype(BF16)  22.1 us
    unnamed x11, local copies, waits for them, and re-layouts  21.1 us
    dot_general x1, matrix products, local(): gate_proj = lax.dot_general(rows, ew[0], nt, preferred_element_type=F32)  10.4 us

profile of v1, /device:TPU:0, one launch (start us, length us, event | category | flops | bytes accessed | tf_op | source)
XLA Modules:
  0.0 314.2 jit_solution(10579188037211114974)
XLA Ops:
  0.6 0.0 copy-start
  0.7 0.7 convert_reduce_fusion.1
  1.3 0.1 copy.25
  1.4 0.0 copy-done
  1.4 1.1 fusion.31
  2.5 1.6 concatenate.3.tok
  4.2 12.0 %copy.21 = bf16[1,3,128,11008]{2,3,1,0:T(8,128)(2,1)} copy(bf16[1,3,128,11008]{3,2,1,0:T(8,128)(2,1)} %param.6) | data formatting | bytes 16908288 | tf_op args[1]
  16.2 175.8 %shard_map.76 = (bf16[3,344,4096]{2,1,0:T(8,128)(2,1)}, bf16[4,4,4,2,16,4224]{5,4,3,2,1,0:T(8,128)(2,1)}, bf16[4,2,1024,128]{3,2,1,0:T(8,128)(2,1)}) custom-call(bf16[3,11008,128]{2,1,0:T(8,128)(2,1)} %bitcast.25, bf16[16,4224]{1,0:T(8,128)(2,1)} %concatenate.3.tok, bf16[2,4096,128]{2,1,0:T(8,128)(2,1)} %bitcast.28), custom_call_target="tpu_custom_call" | custom-call | tf_op jit(solution)/shard_map/pallas_call | solution.py:194
  192.0 2.0 convert_reduce_fusion
  194.1 0.9 multiply_convert_fusion
  194.9 1.4 fusion.33
  196.4 0.4 constant_dynamic-slice_fusion
  196.7 0.2 copy.32
  197.0 0.2 copy.30
  197.2 10.4 %fusion.2 = f32[2048,344]{0,1:T(8,128)S(1)} fusion(bf16[2048,4224]{1,0:T(8,128)(2,1)} %bitcast.30, bf16[3,344,4096]{2,1,0:T(8,128)(2,1)} %get-tuple-element.7), kind=kOutput, calls=%fused_computation.3 | convolution fusion | flops 5771362304 | bytes 22413312 | tf_op jit(solution)/shard_map/dot_general | solution.py:364
  207.6 22.1 %convolution_convert_fusion = bf16[2048,4096]{1,0:T(8,128)(2,1)} fusion(bf16[3,344,4096]{2,1,0:T(8,128)(2,1)} %get-tuple-element.7, bf16[2048,4224]{1,0:T(8,128)(2,1)} %bitcast.31, f32[2048,344]{0,1:T(8,128)S(1)} %fusion.2, f32[2048]{0:T(1024)S(1)} %bitcast.32), kind=kOutput, calls=%fused_computation | convolution fusion | flops 11556044800 | bytes 42016768 | tf_op jit(solution)/shard_map/dot_general | solution.py:367
  229.7 75.8 %shard_map.77 = bf16[16,4096]{1,0:T(8,128)(2,1)} custom-call(bf16[4,4,4,2,16,4096]{5,4,3,2,1,0:T(8,128)(2,1)} %bitcast.26), custom_call_target="tpu_custom_call" | custom-call | tf_op jit(solution)/shard_map/pallas_call | solution.py:328
  305.5 0.0 copy-start.2
  305.5 0.0 copy-start.1
  305.5 8.0 %copy.35 = bf16[1,3,4096,344]{2,3,1,0:T(8,128)(2,1)} copy(bf16[1,3,4096,344]{2,3,1,0:T(8,128)(2,1)} %bitcast.27) | data formatting | bytes 16908288
  313.5 0.0 copy-done.2
  313.5 0.7 copy.36
  314.2 0.0 copy-done.1
  (2 shorter events, 0.0 us)
Async XLA Ops:
  0.6 0.8 copy-start
  305.5 8.0 %copy-start.2 = (bf16[16,4096]{1,0:T(8,128)(2,1)S(1)}, bf16[16,4096]{1,0:T(8,128)(2,1)}, u32[]{:S(2)}) copy-start(bf16[16,4096]{1,0:T(8,128)(2,1)} %shard_map.77) | copy-start | bytes 393220
  305.5 8.7 %copy-start.1 = (bf16[4096,4]{0,1:T(4,128)(2,1)S(1)}, bf16[4096,4]{0,1:T(4,128)(2,1)}, u32[]{:S(2)}) copy-start(bf16[4096,4]{0,1:T(4,128)(2,1)} %param.9) | copy-start | bytes 98308

commit v2 on v1

v2 whole, which is shorter than its diff:
```python
import jax
import jax.numpy as jnp
from jax import lax
from jax.experimental import pallas as pl
from jax.experimental.pallas import tpu as pltpu
from jax.sharding import Mesh
from jax.sharding import PartitionSpec as P

MESH = pl.DeviceIdType.MESH
BF16 = jnp.bfloat16
F32 = jnp.float32

PATHS = (("zh", "x", "y"), ("y", "zh", "x"), ("x", "y", "zh"))
SIZE = {"y": 4, "x": 4, "zh": 2}
GRID = ("y", "x", "zh")
ORDERS = (("x", "y", "z"), ("y", "z", "x"), ("z", "x", "y"))


class Place:
    def __init__(self):
        self.y, self.x = lax.axis_index("y"), lax.axis_index("x")
        self.zh, self.zl = lax.axis_index("zh"), lax.axis_index("zl")
        self.core = lax.axis_index("core")
        self.z = self.zh * 2 + self.zl
        self.at = {"x": self.x, "y": self.y, "z": self.z}

    def shift(self, axis, k):
        return lax.rem(self.at[axis] + k, 4)

    def along(self, axis, k):
        v = self.shift(axis, k)
        if axis == "z":
            return {"zh": v // 2, "zl": lax.rem(v, 2)}
        return {axis: v}

    def shard(self, o):
        return lax.rem(self.y + o[0], 4), lax.rem(self.x + o[1], 4), lax.rem(self.zh + o[2], 2)


def block_index(place, order, phase, coords=None):
    done = order[:phase]
    out = []
    for axis in ("z", "y", "x"):
        if axis in done:
            out.append(slice(None))
        else:
            out.append(place.at[axis] if coords is None or axis not in coords else coords[axis])
    return tuple(out)


def gather_kernel(wt, tok, att, ew, tall, arecv, b1, b2, tbuf, abuf,
                  s1, r1, s2, r2, s3, r3, gs, gr, cs, cr, as_, ar, ls):
    p = Place()
    branch = p.zl * 2 + p.core
    rows = att.shape[1] // 4
    third = tok.shape[1] // 3
    pos = {"y": p.y, "x": p.x, "zh": p.zh}

    def near(axis, k):
        return lax.rem(pos[axis] + k, SIZE[axis])

    bar = pltpu.get_barrier_semaphore()
    peers = [p.along(a, k) for a in ("x", "y", "z") for k in (1, 2, 3)]
    peers += [{"core": 1 - p.core}, {"zl": 1 - p.zl, "core": 1 - p.core}]
    for q in peers:
        pl.semaphore_signal(bar, inc=1, device_id=q, device_id_type=MESH)
    pl.semaphore_wait(bar, len(peers))

    def start(copies):
        for cp in copies:
            cp.start()

    def lanes(c):
        return pl.ds(c * third, third)

    def gather_copies(phase):
        out = []
        for c, order in enumerate(ORDERS):
            dst = tall.at[(p.core,) + block_index(p, order, phase) + (slice(None), lanes(c))]
            src = tok.at[:, lanes(c)] if phase == 0 else dst
            for k in (1, 3, 2):
                i = (phase * 3 + c) * 3 + k - 1
                out.append(
                    pltpu.make_async_remote_copy(
                        src, dst, gs.at[i], gr.at[i],
                        device_id=p.along(order[phase], k), device_id_type=MESH,
                    )
                )
        return out

    def att_copies():
        out = []
        for j, (dz, dc) in enumerate(((1, 0), (1, 1), (0, 1))):
            z2 = lax.rem(p.zl + dz, 2)
            c2 = lax.rem(p.core + dc, 2)
            b2_ = z2 * 2 + c2
            out.append(
                pltpu.make_async_remote_copy(
                    att.at[:, pl.ds(pl.multiple_of(b2_ * rows, 8), rows), :],
                    arecv.at[j], as_.at[j], ar.at[j],
                    device_id={"zl": z2, "core": c2}, device_id_type=MESH,
                )
            )
        return out

    def blocks(ref, **fixed):
        return ref.at[tuple(fixed.get(a, slice(None)) for a in GRID)]

    def remote(src, dst, send, recv, axis, k):
        return pltpu.make_async_remote_copy(
            src, dst, send, recv, device_id={axis: near(axis, k)}, device_id_type=MESH
        )

    def hops(axis):
        return (1, 3, 2) if SIZE[axis] == 4 else (1,)

    def column(ref, m, y, x, zh):
        lane = ((y * 4 + x) * 2 + zh) * 128
        return ref.at[m, :, pl.ds(pl.multiple_of(lane, 128), 128)]

    step1, step2, step3, keep = {}, {}, {}, []
    number2 = number3 = 0
    for m, (a, b, c) in enumerate(PATHS):
        for k in hops(a):
            step1[m, k] = remote(
                blocks(wt.at[m], **{a: near(a, k)}), blocks(b1.at[m], **{a: pos[a]}),
                s1.at[m * 3 + k - 1], r1.at[m * 3 + k - 1], a, k,
            )
        for i in range(SIZE[a]):
            src_a = near(a, SIZE[a] - i)
            for k in hops(b):
                step2[m, i, k] = remote(
                    blocks(b1.at[m], **{a: src_a, b: near(b, k)}),
                    blocks(b2.at[m], **{a: src_a, b: pos[b]}),
                    s2.at[number2], r2.at[number2], b, k,
                )
                number2 += 1
            for j in range(SIZE[b]):
                src_b = near(b, SIZE[b] - j)
                held = b1 if j == 0 else b2
                for k in hops(c):
                    step3[m, i, j, k] = remote(
                        blocks(held.at[m], **{a: src_a, b: src_b, c: near(c, k)}),
                        column(ew, m, **{a: src_a, b: src_b, c: pos[c]}),
                        s3.at[number3], r3.at[number3], c, k,
                    )
                    number3 += 1
                keep.append(
                    (m, i, j, pltpu.make_async_copy(
                        blocks(held.at[m], **{a: src_a, b: src_b, c: pos[c]}),
                        column(ew, m, **{a: src_a, b: src_b, c: pos[c]}),
                        ls.at[10 + len(keep)],
                    ))
                )
    keep = {(m, i, j): cp for m, i, j, cp in keep}

    phases = [gather_copies(ph) for ph in range(3)]
    swap = [
        pltpu.make_async_remote_copy(
            tall.at[p.core, :, :, :, :, lanes(c)], tall.at[p.core, :, :, :, :, lanes(c)],
            cs.at[c], cr.at[c], device_id={"core": 1 - p.core}, device_id_type=MESH,
        )
        for c in range(3)
    ]
    acopies = att_copies()

    start(phases[0])
    start(step1.values())
    start(acopies)

    local_in = [
        pltpu.make_async_copy(blocks(wt.at[m], **{a: pos[a]}), blocks(b1.at[m], **{a: pos[a]}), ls.at[m])
        for m, (a, _, _) in enumerate(PATHS)
    ]
    own = [
        (tok, tbuf, tall.at[p.core, p.z, p.y, p.x]),
        (att.at[:, pl.ds(pl.multiple_of(branch * rows, 8), rows), :], abuf, arecv.at[3]),
    ]
    ins = [pltpu.make_async_copy(s, v, ls.at[3 + i]) for i, (s, v, _) in enumerate(own)]
    outs = [pltpu.make_async_copy(v, d, ls.at[5 + i]) for i, (_, v, d) in enumerate(own)]
    start(local_in)
    start(ins)
    for i in range(2):
        ins[i].wait()
        outs[i].start()
    for cp in local_in + outs:
        cp.wait()

    for cp in phases[0]:
        cp.wait()
    start(phases[1])
    for m in range(3):
        start(step2[m, 0, k] for k in hops(PATHS[m][1]))
    for i in (1, 3, 2):
        for m in range(3):
            if i in hops(PATHS[m][0]):
                step1[m, i].wait()
                start(step2[m, i, k] for k in hops(PATHS[m][1]))
        if i == 1:
            for cp in phases[1]:
                cp.wait()
            start(phases[2])
    for i in (0, 1, 3, 2):
        for m in range(3):
            if i < SIZE[PATHS[m][0]]:
                start(step3[m, i, 0, k] for k in hops(PATHS[m][2]))
                keep[m, i, 0].start()
    for i in (0, 1, 3, 2):
        for j in (1, 3, 2):
            for m in range(3):
                if i < SIZE[PATHS[m][0]] and j in hops(PATHS[m][1]):
                    step2[m, i, j].wait()
                    start(step3[m, i, j, k] for k in hops(PATHS[m][2]))
                    keep[m, i, j].start()
        if i == 1:
            for cp in phases[2]:
                cp.wait()
            start(swap)
    for cp in acopies + swap + list(keep.values()) + list(step3.values()):
        cp.wait()


def gather(wt, tok, att):
    units, depth = wt.shape[4:]
    rows = att.shape[1] // 4
    dma = pltpu.SemaphoreType.DMA
    return pl.pallas_call(
        gather_kernel,
        out_shape=(
            jax.ShapeDtypeStruct((3, units, depth * 32), BF16),
            jax.ShapeDtypeStruct((2, 4, 4, 4) + tok.shape, BF16),
            jax.ShapeDtypeStruct((4, 2, rows, att.shape[2]), BF16),
        ),
        in_specs=[pl.BlockSpec(memory_space=pl.ANY)] * 3,
        out_specs=[pl.BlockSpec(memory_space=pl.ANY)] * 3,
        scratch_shapes=[
            pltpu.VMEM(wt.shape, BF16),
            pltpu.VMEM(wt.shape, BF16),
            pltpu.VMEM(tok.shape, BF16),
            pltpu.VMEM((2, rows, att.shape[2]), BF16),
            dma((9,)), dma((9,)), dma((24,)), dma((24,)), dma((64,)), dma((64,)),
            dma((27,)), dma((27,)), dma((3,)), dma((3,)), dma((3,)), dma((3,)), dma((48,)),
        ],
        compiler_params=pltpu.CompilerParams(
            collective_id=0, has_side_effects=True, vmem_limit_bytes=40 * 1024 * 1024
        ),
    )(wt, tok, att)


def colour_lanes(width):
    tiles = width // 128
    cut = [0, -(-tiles // 3), -(-tiles // 3) + (tiles - tiles // 3) // 2, tiles]
    return [(cut[i] * 128, (cut[i + 1] - cut[i]) * 128) for i in range(3)]


def hidden_kernel(rows, ew, hid, copy, wv, sems):
    step = pl.program_id(0)
    units, width = ew.shape[1:]
    loads = [pltpu.make_async_copy(ew.at[m], wv.at[m, pl.ds(0, units)], sems.at[m]) for m in range(3)]
    stores = [pltpu.make_async_copy(wv.at[m, pl.ds(0, units)], copy.at[m], sems.at[3 + m]) for m in range(3)]

    @pl.when(step == 0)
    def _():
        for cp in loads:
            cp.start()
        for m in range(3):
            loads[m].wait()
            stores[m].start()

    both = wv[0:2].reshape(2 * wv.shape[1], width)
    proj = lax.dot_general(
        rows[:, :width], both, (((1,), (1,)), ((), ())), preferred_element_type=F32
    )
    gate, up = proj[:, :wv.shape[1]], proj[:, wv.shape[1]:]
    extra = rows[:, width:].astype(F32)
    lane = lax.broadcasted_iota(jnp.int32, extra.shape, 1)
    expert = lax.axis_index("zl") * 2 + lax.axis_index("core")
    mine = (lane == expert) | (lane == expert + 4)
    weight = jnp.sum(jnp.where(mine, extra, 0.0), axis=1, keepdims=True)
    value = gate / (1.0 + jnp.exp(-gate)) * up * weight
    hid[...] = value[:, :units].astype(BF16)

    @pl.when(step == pl.num_programs(0) - 1)
    def _():
        for cp in stores:
            cp.wait()


def hidden_of(rows, ew):
    count, units = 256, ew.shape[1]
    return pl.pallas_call(
        hidden_kernel,
        grid=(rows.shape[0] // count,),
        out_shape=(
            jax.ShapeDtypeStruct((rows.shape[0], units), BF16),
            jax.ShapeDtypeStruct(ew.shape, BF16),
        ),
        in_specs=[
            pl.BlockSpec((count, rows.shape[1]), lambda i: (i, 0)),
            pl.BlockSpec(memory_space=pl.ANY),
        ],
        out_specs=[
            pl.BlockSpec((count, units), lambda i: (i, 0)),
            pl.BlockSpec(memory_space=pl.ANY),
        ],
        scratch_shapes=[
            pltpu.VMEM((3, -(-units // 128) * 128, ew.shape[2]), BF16),
            pltpu.SemaphoreType.DMA((6,)),
        ],
        compiler_params=pltpu.CompilerParams(vmem_limit_bytes=40 * 1024 * 1024),
    )(rows, ew)


CHUNKS = (1, 3, 2, 0)


def scatter_kernel(hid, ew, out, down, snd, r0, s0, r1, s1, r2, s2, r3, xs, xr, ss, rs, ls):
    p = Place()
    load = pltpu.make_async_copy(ew.at[2], down, ls)
    load.start()
    bar = pltpu.get_barrier_semaphore()
    peers = [{"core": 1 - p.core}] + [p.along(a, k) for a in ("x", "y", "z") for k in (1, 2, 3)]
    for q in peers:
        pl.semaphore_signal(bar, inc=1, device_id=q, device_id_type=MESH)
    pl.semaphore_wait(bar, len(peers))
    load.wait()
    cuts = colour_lanes(down.shape[1])

    def product(core, z, c):
        lo, n = cuts[c]
        rows = hid[core, z].reshape(-1, hid.shape[-1])
        value = jnp.dot(rows, down[:, lo:lo + n], preferred_element_type=F32)
        return value.reshape(4, 4, -1, n)

    def swap(j, c):
        z = p.shift("z", j)
        return pltpu.make_async_remote_copy(
            snd[c].at[z], r0[c].at[z], xs.at[j * 3 + c], xr.at[j * 3 + c],
            device_id={"core": 1 - p.core}, device_id_type=MESH,
        )

    swaps = {(j, c): swap(j, c) for j in range(4) for c in range(3)}
    number = iter(range(60))

    def remote(src, dst, axis, k):
        i = next(number)
        return pltpu.make_async_remote_copy(
            src, dst, ss.at[i], rs.at[i], device_id=p.along(axis, k), device_id_type=MESH
        )

    def give(j):
        z = p.shift("z", j)
        for c in range(3):
            snd[c][z] = product(1 - p.core, z, c).astype(BF16)
            swaps[j, c].start()

    stage1 = [[], [], []]

    def take(j):
        z = p.shift("z", j)
        for c, order in enumerate(ORDERS):
            value = product(p.core, z, c)
            swaps[j, c].wait()
            s0[c][z] = (value + r0[c][z].astype(F32)).astype(BF16)
            axis = order[0]
            if axis == "z":
                copies = [remote(s0[c].at[z], r1[c].at[j - 1], "z", j)] if j else []
            elif axis == "y":
                copies = [
                    remote(s0[c].at[z, p.shift("y", k)], r1[c].at[k - 1, z], "y", k) for k in (1, 3, 2)
                ]
            else:
                copies = [
                    remote(s0[c].at[z, :, p.shift("x", k)], r1[c].at[k - 1, z], "x", k) for k in (1, 3, 2)
                ]
            for cp in copies:
                cp.start()
            stage1[c] += copies

    give(CHUNKS[0])
    for n in range(4):
        if n < 3:
            give(CHUNKS[n + 1])
        take(CHUNKS[n])

    def pick(ref, left, axis, v):
        return ref.at[tuple(v if a == axis else slice(None) for a in left)]

    def left_after(order, phase):
        return [a for a in ("z", "y", "x") if a not in order[:phase]]

    def send(c, axis, src_of, dst):
        copies = [remote(src_of(p.shift(axis, k)), dst.at[k - 1], axis, k) for k in (1, 3, 2)]
        for cp in copies:
            cp.start()
        return copies

    stage2, stage3 = [], []
    for c, order in enumerate(ORDERS):
        for cp in stage1[c]:
            cp.wait()
        mine = pick(s0[c], left_after(order, 0), order[0], p.at[order[0]])

        def add(i, carry, c=c, mine=mine):
            at = (i // 4, lax.rem(i, 4))
            total = mine[at].astype(F32)
            for k in range(3):
                total += r1[c][(k,) + at].astype(F32)
            s1[c][at] = total.astype(BF16)
            return carry

        lax.fori_loop(0, 16, add, 0)
        left = left_after(order, 1)
        stage2.append(send(c, order[1], lambda v, c=c, left=left, a=order[1]: pick(s1[c], left, a, v), r2[c]))

    for c, order in enumerate(ORDERS):
        for cp in stage2[c]:
            cp.wait()
        mine = pick(s1[c], left_after(order, 1), order[1], p.at[order[1]])

        def add(i, carry, c=c, mine=mine):
            total = mine[i].astype(F32)
            for k in range(3):
                total += r2[c][k, i].astype(F32)
            s2[c][i] = total.astype(BF16)
            return carry

        lax.fori_loop(0, 4, add, 0)
        left = left_after(order, 2)
        stage3.append(send(c, order[2], lambda v, c=c, left=left, a=order[2]: pick(s2[c], left, a, v), r3[c]))

    for c, order in enumerate(ORDERS):
        for cp in stage3[c]:
            cp.wait()
        total = s2[c][p.at[order[2]]].astype(F32)
        for k in range(3):
            total += r3[c][k].astype(F32)
        lo, n = cuts[c]
        out[:, lo:lo + n] = total.astype(BF16)


def scatter(hid, ew):
    rows, units = hid.shape[-2:]
    width = ew.shape[2]
    cuts = colour_lanes(width)
    dma = pltpu.SemaphoreType.DMA

    def bufs(*lead):
        return [pltpu.VMEM(lead + (rows, n), BF16) for _, n in cuts]

    return pl.pallas_call(
        scatter_kernel,
        out_shape=jax.ShapeDtypeStruct((rows, width), BF16),
        in_specs=[pl.BlockSpec(memory_space=pltpu.VMEM), pl.BlockSpec(memory_space=pl.ANY)],
        out_specs=pl.BlockSpec(memory_space=pltpu.VMEM),
        scratch_shapes=[
            pltpu.VMEM((units, width), BF16),
            bufs(4, 4, 4), bufs(4, 4, 4), bufs(4, 4, 4),
            bufs(3, 4, 4), bufs(4, 4), bufs(3, 4), bufs(4), bufs(3),
            dma((12,)), dma((12,)), dma((60,)), dma((60,)), dma,
        ],
        compiler_params=pltpu.CompilerParams(
            collective_id=1, has_side_effects=True, vmem_limit_bytes=56 * 1024 * 1024
        ),
    )(hid, ew)


def local(attention_weights, ffn_weights, tokens, routes, router):
    experts = router.shape[1]
    width = tokens.shape[1]
    wt = jnp.swapaxes(ffn_weights[0], 1, 2)
    wt = wt.reshape(3, 4, 4, 2, wt.shape[1] // 32, wt.shape[2])
    gates = jax.nn.sigmoid(jnp.dot(tokens, router, preferred_element_type=F32))
    named = jnp.sum((routes[:, :, None] == jnp.arange(experts, dtype=jnp.int32)).astype(F32), axis=1)
    weighting = named * gates
    high = lax.reduce_precision(weighting, 8, 7)
    low = (weighting - high).astype(BF16)
    high = high.astype(BF16)
    tok = jnp.concatenate(
        [tokens, high, low, jnp.zeros((tokens.shape[0], 128 - 2 * experts), BF16)], axis=1
    )
    ew, tall, arecv = gather(wt, tok, attention_weights[0])
    flat = tall.reshape(-1, tok.shape[1])
    hid, kept = hidden_of(flat, ew)
    mixed_output = scatter(hid.reshape(2, 4, 4, 4, tokens.shape[0], -1), kept)
    merged = (jnp.sum(arecv.astype(F32), axis=0) * 0.25).astype(BF16)
    return merged, jnp.swapaxes(kept, 1, 2)[None], mixed_output


def solution(mesh):
    torus = Mesh(mesh.devices.reshape(2, 2, 4, 4, 2), ("zl", "core", "y", "x", "zh"))
    shard = ("y", "x", "zh")
    branch = ("zl", "core")
    in_specs = (
        P(branch, None, None, shard),
        P(branch, None, shard, None),
        P(branch + shard, None),
        P(branch + shard, None),
        P(),
    )
    out_specs = (P(None, branch, shard), P(branch, None, None, shard), P(branch + shard, None))
    return jax.shard_map(local, mesh=torus, in_specs=in_specs, out_specs=out_specs, check_vma=False)
```

time: 315 us -> 263 us (0.83)
  matrix products: 33.6 us -> 1.08 us
  Pallas kernels: 252 us -> 243 us
  local copies, waits for them, and re-layouts: 24.6 us -> 16 us
    dot_general x2 -> x0, matrix products: 32.5 us -> none  [the longest x1 22.1 us: local(): part = jnp.dot(hidden, ew[2], preferred_element_type=F32).astype(BF16)]
    pallas_call x0 -> x1, Pallas kernels: none -> 18.7 us  [hidden_of(): pl.pallas_call(hidden_kernel, grid=(rows.shape[0] // count,), out_shape=(...]
    unnamed x11 -> x7, local copies, waits for them, and re-layouts: 21.1 us -> 2.73 us
    pallas_call x1, Pallas kernels: 75.8 us -> 60.1 us  [scatter(): pl.pallas_call(scatter_kernel, out_shape=jax.ShapeDtypeStruct((rows, widt...]
    transpose x0 -> x1, local copies, waits for them, and re-layouts: none -> 12.2 us  [local(): wt = jnp.swapaxes(ffn_weights[0], 1, 2)]
    pallas_call x1, Pallas kernels: 176 us -> 164 us  [gather(): pl.pallas_call(gather_kernel, out_shape=(jax.ShapeDtypeStruct((3, units,...]
where the time goes in v2:
time: 263 us; the launch traced here: 262 us
  Pallas kernels  243 us (92%)
  local copies, waits for them, and re-layouts  16 us (6%)
    pallas_call x1, Pallas kernels, gather(): pl.pallas_call(gather_kernel, out_shape=(jax.ShapeDtypeStruct((3, units,...  164 us
    pallas_call x1, Pallas kernels, scatter(): pl.pallas_call(scatter_kernel, out_shape=jax.ShapeDtypeStruct((rows, widt...  60.1 us
    pallas_call x1, Pallas kernels, hidden_of(): pl.pallas_call(hidden_kernel, grid=(rows.shape[0] // count,), out_shape=(...  18.7 us
    transpose x1, local copies, waits for them, and re-layouts, local(): wt = jnp.swapaxes(ffn_weights[0], 1, 2)  12.2 us

profile of v2, /device:TPU:0, one launch (start us, length us, event | category | flops | bytes accessed | tf_op | source)
XLA Modules:
  0.0 262.4 jit_solution(16360413546312354600)
XLA Ops:
  0.6 0.0 copy-start
  0.6 0.7 convert_reduce_fusion.1
  1.3 0.1 copy.18
  1.4 0.0 copy-done
  1.4 1.1 fusion.4
  2.5 1.0 concatenate.3.tok
  3.5 0.0 copy-start.1
  3.5 12.2 %copy.14 = bf16[3,11008,128]{2,1,0:T(8,128)(2,1)} copy(bf16[3,11008,128]{1,2,0:T(8,128)(2,1)} %bitcast.16) | data formatting | bytes 16908288 | tf_op jit(solution)/shard_map/transpose | solution.py:471
  15.7 0.0 copy-done.1
  15.7 164.0 %shard_map.76 = (bf16[3,344,4096]{2,1,0:T(8,128)(2,1)S(1)}, bf16[2,4,4,4,16,4224]{5,4,3,2,1,0:T(8,128)(2,1)}, bf16[4,2,1024,128]{3,2,1,0:T(8,128)(2,1)S(1)}) custom-call(bf16[3,4,4,2,344,128]{5,4,3,2,1,0:T(8,128)(2,1)} %bitcast.14, bf16[16,4224]{1,0:T(8,128)(2,1)S(1)} %concatenate.3.tok, bf16[2,4096,128]{2,1,0:T(8,128)(2,1)S(1)} %bitcast.12), custom_call_target="tpu_custom_call" | custom-call | tf_op jit(solution)/shard_map/pallas_call | solution.py:227
  179.7 0.3 convert_reduce_fusion
  180.0 0.9 multiply_convert_fusion
  180.9 18.7 %shard_map.77 = (bf16[2048,344]{1,0:T(8,128)(2,1)S(1)}, bf16[3,344,4096]{2,1,0:T(8,128)(2,1)}) custom-call(bf16[2048,4224]{1,0:T(8,128)(2,1)} %bitcast.15, bf16[3,344,4096]{2,1,0:T(8,128)(2,1)S(1)} %get-tuple-element.10.ew), custom_call_target="tpu_custom_call" | custom-call | tf_op jit(solution)/shard_map/pallas_call | solution.py:291
  199.6 0.0 copy-start.2
  199.7 1.1 copy-done.2
  200.8 60.1 %shard_map.78 = bf16[16,4096]{1,0:T(8,128)(2,1)} custom-call(bf16[2,4,4,4,16,344]{5,4,3,2,1,0:T(8,128)(2,1)} %bitcast.13, bf16[3,344,4096]{2,1,0:T(8,128)(2,1)} %get-tuple-element.11.ew), custom_call_target="tpu_custom_call" | custom-call | tf_op jit(solution)/shard_map/pallas_call | solution.py:451
  260.9 1.6 copy.21
  (1 shorter events, 0.0 us)
Async XLA Ops:
  0.6 0.8 copy-start
  3.5 12.2 %copy-start.1 = (bf16[1,2,4096,128]{3,2,1,0:T(8,128)(2,1)S(1)}, bf16[1,2,4096,128]{3,2,1,0:T(8,128)(2,1)}, u32[]{:S(2)}) copy-start(bf16[1,2,4096,128]{3,2,1,0:T(8,128)(2,1)} %param.5) | copy-start | bytes 6291460
  199.6 1.2 copy-start.2

commit v3 on v2

--- a/solution.py
+++ b/solution.py
@@ -48,37 +48,50 @@
     return tuple(out)
 
 
-def gather_kernel(wt, tok, att, ew, tall, arecv, b1, b2, tbuf, abuf,
+def gather_kernel(w, tok, att, ew, tall, near_sum, far_sum, raw, wt, b1, b2, turned, tbuf, aown, arecv,
                   s1, r1, s2, r2, s3, r3, gs, gr, cs, cr, as_, ar, ls):
     p = Place()
-    branch = p.zl * 2 + p.core
     rows = att.shape[1] // 4
     third = tok.shape[1] // 3
+    units = ew.shape[1]
     pos = {"y": p.y, "x": p.x, "zh": p.zh}
 
     def near(axis, k):
         return lax.rem(pos[axis] + k, SIZE[axis])
 
+    def start(copies):
+        for cp in copies:
+            cp.start()
+
+    loads = [pltpu.make_async_copy(w.at[m], raw.at[m], ls.at[m]) for m in range(3)]
+    tin = pltpu.make_async_copy(tok, tbuf, ls.at[3])
+    tout = pltpu.make_async_copy(tbuf, tall.at[p.core, p.z, p.y, p.x], ls.at[4])
+    tin.start()
+    start(loads)
+    ours = [
+        pltpu.make_async_copy(
+            att.at[:, pl.ds(pl.multiple_of((z * 2 + p.core) * rows, 8), rows), :], aown.at[z], ls.at[45 + z]
+        )
+        for z in range(2)
+    ]
+    start(ours)
+
     bar = pltpu.get_barrier_semaphore()
     peers = [p.along(a, k) for a in ("x", "y", "z") for k in (1, 2, 3)]
-    peers += [{"core": 1 - p.core}, {"zl": 1 - p.zl, "core": 1 - p.core}]
+    peers += [{"core": 1 - p.core}]
     for q in peers:
         pl.semaphore_signal(bar, inc=1, device_id=q, device_id_type=MESH)
     pl.semaphore_wait(bar, len(peers))
 
-    def start(copies):
-        for cp in copies:
-            cp.start()
-
     def lanes(c):
         return pl.ds(c * third, third)
 
-    def gather_copies(phase):
+    def gather_copies(phase, hops_):
         out = []
         for c, order in enumerate(ORDERS):
             dst = tall.at[(p.core,) + block_index(p, order, phase) + (slice(None), lanes(c))]
             src = tok.at[:, lanes(c)] if phase == 0 else dst
-            for k in (1, 3, 2):
+            for k in hops_:
                 i = (phase * 3 + c) * 3 + k - 1
                 out.append(
                     pltpu.make_async_remote_copy(
@@ -88,17 +101,19 @@
                 )
         return out
 
-    def att_copies():
+    def relay_copies(back):
         out = []
-        for j, (dz, dc) in enumerate(((1, 0), (1, 1), (0, 1))):
-            z2 = lax.rem(p.zl + dz, 2)
-            c2 = lax.rem(p.core + dc, 2)
-            b2_ = z2 * 2 + c2
+        for c, order in enumerate(ORDERS):
+            axis = order[2]
+            at = list(block_index(p, order, 2, {axis: p.shift(axis, 4 - back)}))
+            split = [n for n in range(3) if isinstance(at[n], slice)][0]
+            at[split] = pl.ds(0 if back == 1 else 2, 2)
+            ref = tall.at[(p.core,) + tuple(at) + (slice(None), lanes(c))]
+            i = 27 + c * 2 + (0 if back == 1 else 1)
             out.append(
                 pltpu.make_async_remote_copy(
-                    att.at[:, pl.ds(pl.multiple_of(b2_ * rows, 8), rows), :],
-                    arecv.at[j], as_.at[j], ar.at[j],
-                    device_id={"zl": z2, "core": c2}, device_id_type=MESH,
+                    ref, ref, gs.at[i], gr.at[i],
+                    device_id=p.along(axis, back), device_id_type=MESH,
                 )
             )
         return out
@@ -118,7 +133,7 @@
         lane = ((y * 4 + x) * 2 + zh) * 128
         return ref.at[m, :, pl.ds(pl.multiple_of(lane, 128), 128)]
 
-    step1, step2, step3, keep = {}, {}, {}, []
+    step1, step2, step3, keep = {}, {}, {}, {}
     number2 = number3 = 0
     for m, (a, b, c) in enumerate(PATHS):
         for k in hops(a):
@@ -128,16 +143,17 @@
             )
         for i in range(SIZE[a]):
             src_a = near(a, SIZE[a] - i)
+            first = wt if i == 0 else b1
             for k in hops(b):
                 step2[m, i, k] = remote(
-                    blocks(b1.at[m], **{a: src_a, b: near(b, k)}),
+                    blocks(first.at[m], **{a: src_a, b: near(b, k)}),
                     blocks(b2.at[m], **{a: src_a, b: pos[b]}),
                     s2.at[number2], r2.at[number2], b, k,
                 )
                 number2 += 1
             for j in range(SIZE[b]):
                 src_b = near(b, SIZE[b] - j)
-                held = b1 if j == 0 else b2
+                held = first if j == 0 else b2
                 for k in hops(c):
                     step3[m, i, j, k] = remote(
                         blocks(held.at[m], **{a: src_a, b: src_b, c: near(c, k)}),
@@ -145,61 +161,95 @@
                         s3.at[number3], r3.at[number3], c, k,
                     )
                     number3 += 1
-                keep.append(
-                    (m, i, j, pltpu.make_async_copy(
-                        blocks(held.at[m], **{a: src_a, b: src_b, c: pos[c]}),
-                        column(ew, m, **{a: src_a, b: src_b, c: pos[c]}),
-                        ls.at[10 + len(keep)],
-                    ))
+                keep[m, i, j] = pltpu.make_async_copy(
+                    blocks(held.at[m], **{a: src_a, b: src_b, c: pos[c]}),
+                    column(ew, m, **{a: src_a, b: src_b, c: pos[c]}),
+                    ls.at[5 + len(keep)],
                 )
-    keep = {(m, i, j): cp for m, i, j, cp in keep}
-
-    phases = [gather_copies(ph) for ph in range(3)]
-    swap = [
+
+    phase0, phase1 = gather_copies(0, (1, 3, 2)), gather_copies(1, (1, 3, 2))
+    phase2a, phase2b = gather_copies(2, (1,)), gather_copies(2, (3,))
+    relay_a, relay_b = relay_copies(1), relay_copies(3)
+    def swap_copies(k):
+        out = []
+        for c, order in enumerate(ORDERS):
+            at = block_index(p, order, 2, {order[2]: p.shift(order[2], 4 - k)})
+            ref = tall.at[(p.core,) + at + (slice(None), lanes(c))]
+            out.append(
+                pltpu.make_async_remote_copy(
+                    ref, ref, cs.at[c * 4 + k], cr.at[c * 4 + k],
+                    device_id={"core": 1 - p.core}, device_id_type=MESH,
+                )
+            )
+        return out
+
+    swaps = [swap_copies(k) for k in range(4)]
+    acopies = [
         pltpu.make_async_remote_copy(
-            tall.at[p.core, :, :, :, :, lanes(c)], tall.at[p.core, :, :, :, :, lanes(c)],
-            cs.at[c], cr.at[c], device_id={"core": 1 - p.core}, device_id_type=MESH,
+            att.at[:, pl.ds(pl.multiple_of((z * 2 + 1 - p.core) * rows, 8), rows), :],
+            arecv.at[z], as_.at[z], ar.at[z],
+            device_id={"core": 1 - p.core}, device_id_type=MESH,
         )
-        for c in range(3)
+        for z in range(2)
     ]
-    acopies = att_copies()
-
-    start(phases[0])
-    start(step1.values())
+
+    start(phase0)
     start(acopies)
-
-    local_in = [
-        pltpu.make_async_copy(blocks(wt.at[m], **{a: pos[a]}), blocks(b1.at[m], **{a: pos[a]}), ls.at[m])
-        for m, (a, _, _) in enumerate(PATHS)
-    ]
-    own = [
-        (tok, tbuf, tall.at[p.core, p.z, p.y, p.x]),
-        (att.at[:, pl.ds(pl.multiple_of(branch * rows, 8), rows), :], abuf, arecv.at[3]),
-    ]
-    ins = [pltpu.make_async_copy(s, v, ls.at[3 + i]) for i, (s, v, _) in enumerate(own)]
-    outs = [pltpu.make_async_copy(v, d, ls.at[5 + i]) for i, (_, v, d) in enumerate(own)]
-    start(local_in)
-    start(ins)
-    for i in range(2):
-        ins[i].wait()
-        outs[i].start()
-    for cp in local_in + outs:
-        cp.wait()
-
-    for cp in phases[0]:
-        cp.wait()
-    start(phases[1])
+    tin.wait()
+    tout.start()
+    tout.wait()
+
+    def turn(m):
+        def body(i, carry):
+            at = pl.ds(pl.multiple_of(i * 256, 256), 256)
+            turned[at, :] = raw[m, :, at].T.astype(F32)
+            return carry
+
+        def place(d, carry):
+            piece = turned[pl.ds(pl.multiple_of(d * units, 8), units), :]
+            wt[m, d // 8, lax.rem(d // 2, 4), lax.rem(d, 2)] = piece.astype(BF16)
+            return carry
+
+        lax.fori_loop(0, raw.shape[2] // 256, body, 0, unroll=2)
+        lax.fori_loop(0, 32, place, 0, unroll=4)
+
+    for m in range(3):
+        loads[m].wait()
+        turn(m)
+        start(step1[m, k] for k in hops(PATHS[m][0]))
+        if m == 0:
+            for cp in phase0:
+                cp.wait()
+            start(phase1)
+        if m == 2:
+            for cp in phase1:
+                cp.wait()
+            start(phase2a)
+            start(phase2b)
+            start(swaps[0])
     for m in range(3):
         start(step2[m, 0, k] for k in hops(PATHS[m][1]))
+    for cp in ours + acopies:
+        cp.wait()
+
+    def pair(i, carry):
+        at = (i // 8, pl.ds(pl.multiple_of(lax.rem(i, 8) * (rows // 8), 16), rows // 8))
+        far = 1 - p.zl
+        near_sum[at] = aown[(p.zl,) + at].astype(F32) + arecv[(p.zl,) + at].astype(F32)
+        far_sum[at] = (aown[(far,) + at].astype(F32) + arecv[(far,) + at].astype(F32)).astype(BF16)
+        return carry
+
+    lax.fori_loop(0, 16, pair, 0)
     for i in (1, 3, 2):
         for m in range(3):
             if i in hops(PATHS[m][0]):
                 step1[m, i].wait()
                 start(step2[m, i, k] for k in hops(PATHS[m][1]))
-        if i == 1:
-            for cp in phases[1]:
-                cp.wait()
-            start(phases[2])
+    for group, relay, k in ((phase2a, relay_a, 1), (phase2b, relay_b, 3)):
+        for cp in group:
+            cp.wait()
+        start(relay)
+        start(swaps[k])
     for i in (0, 1, 3, 2):
         for m in range(3):
             if i < SIZE[PATHS[m][0]]:
@@ -213,38 +263,45 @@
                     start(step3[m, i, j, k] for k in hops(PATHS[m][2]))
                     keep[m, i, j].start()
         if i == 1:
-            for cp in phases[2]:
+            for cp in relay_a + relay_b:
                 cp.wait()
-            start(swap)
-    for cp in acopies + swap + list(keep.values()) + list(step3.values()):
+            start(swaps[2])
+    for cp in sum(swaps, []) + list(keep.values()) + list(step3.values()):
         cp.wait()
 
 
-def gather(wt, tok, att):
-    units, depth = wt.shape[4:]
+def gather(w, tok, att):
+    units = w.shape[2] // 32
+    depth = w.shape[1]
     rows = att.shape[1] // 4
     dma = pltpu.SemaphoreType.DMA
+    split = (3, 4, 4, 2, units, depth)
     return pl.pallas_call(
         gather_kernel,
         out_shape=(
             jax.ShapeDtypeStruct((3, units, depth * 32), BF16),
             jax.ShapeDtypeStruct((2, 4, 4, 4) + tok.shape, BF16),
-            jax.ShapeDtypeStruct((4, 2, rows, att.shape[2]), BF16),
+            jax.ShapeDtypeStruct((2, rows, att.shape[2]), F32),
+            jax.ShapeDtypeStruct((2, rows, att.shape[2]), BF16),
         ),
         in_specs=[pl.BlockSpec(memory_space=pl.ANY)] * 3,
-        out_specs=[pl.BlockSpec(memory_space=pl.ANY)] * 3,
+        out_specs=[pl.BlockSpec(memory_space=pl.ANY)] * 2 + [pl.BlockSpec(memory_space=pltpu.VMEM)] * 2,
         scratch_shapes=[
-            pltpu.VMEM(wt.shape, BF16),
-            pltpu.VMEM(wt.shape, BF16),
+            pltpu.VMEM(w.shape, BF16),
+            pltpu.VMEM(split, BF16),
+            pltpu.VMEM(split, BF16),
+            pltpu.VMEM(split, BF16),
+            pltpu.VMEM((w.shape[2], depth), F32),
             pltpu.VMEM(tok.shape, BF16),
-            pltpu.VMEM((2, rows, att.shape[2]), BF16),
+            pltpu.VMEM((2, 2, rows, att.shape[2]), BF16),
+            pltpu.VMEM((2, 2, rows, att.shape[2]), BF16),
             dma((9,)), dma((9,)), dma((24,)), dma((24,)), dma((64,)), dma((64,)),
-            dma((27,)), dma((27,)), dma((3,)), dma((3,)), dma((3,)), dma((3,)), dma((48,)),
+            dma((33,)), dma((33,)), dma((12,)), dma((12,)), dma((2,)), dma((2,)), dma((48,)),
         ],
         compiler_params=pltpu.CompilerParams(
-            collective_id=0, has_side_effects=True, vmem_limit_bytes=40 * 1024 * 1024
+            collective_id=0, has_side_effects=True, vmem_limit_bytes=56 * 1024 * 1024
         ),
-    )(wt, tok, att)
+    )(w, tok, att)
 
 
 def colour_lanes(width):
@@ -253,77 +310,103 @@
     return [(cut[i] * 128, (cut[i + 1] - cut[i]) * 128) for i in range(3)]
 
 
-def hidden_kernel(rows, ew, hid, copy, wv, sems):
-    step = pl.program_id(0)
-    units, width = ew.shape[1:]
-    loads = [pltpu.make_async_copy(ew.at[m], wv.at[m, pl.ds(0, units)], sems.at[m]) for m in range(3)]
-    stores = [pltpu.make_async_copy(wv.at[m, pl.ds(0, units)], copy.at[m], sems.at[3 + m]) for m in range(3)]
-
-    @pl.when(step == 0)
-    def _():
-        for cp in loads:
-            cp.start()
-        for m in range(3):
-            loads[m].wait()
-            stores[m].start()
-
-    both = wv[0:2].reshape(2 * wv.shape[1], width)
+def hidden_block(rows, weights):
+    padded, width = weights.shape[1:]
+    rows = rows.reshape(-1, rows.shape[-1])
     proj = lax.dot_general(
-        rows[:, :width], both, (((1,), (1,)), ((), ())), preferred_element_type=F32
+        rows[:, :width], weights[...].reshape(2 * padded, width), (((1,), (1,)), ((), ())),
+        preferred_element_type=F32,
     )
-    gate, up = proj[:, :wv.shape[1]], proj[:, wv.shape[1]:]
+    gate, up = proj[:, :padded], proj[:, padded:]
     extra = rows[:, width:].astype(F32)
     lane = lax.broadcasted_iota(jnp.int32, extra.shape, 1)
     expert = lax.axis_index("zl") * 2 + lax.axis_index("core")
     mine = (lane == expert) | (lane == expert + 4)
     weight = jnp.sum(jnp.where(mine, extra, 0.0), axis=1, keepdims=True)
-    value = gate / (1.0 + jnp.exp(-gate)) * up * weight
-    hid[...] = value[:, :units].astype(BF16)
-
-    @pl.when(step == pl.num_programs(0) - 1)
-    def _():
-        for cp in stores:
-            cp.wait()
+    return (gate / (1.0 + jnp.exp(-gate)) * up * weight).astype(BF16)
+
+
+def hidden_kernel(rows, ew, hid, copy, x, wv, down, held, sems):
+    p = Place()
+    units = ew.shape[1]
+    first = p.shift("z", CHUNKS[0])
+    spots = [wv.at[0, pl.ds(0, units)], wv.at[1, pl.ds(0, units)], down]
+    xin = [pltpu.make_async_copy(rows.at[h, first], x.at[h], sems.at[6 + h]) for h in range(2)]
+    loads = [pltpu.make_async_copy(ew.at[m], spots[m], sems.at[m]) for m in range(3)]
+    stores = [pltpu.make_async_copy(spots[m], copy.at[m], sems.at[3 + m]) for m in range(3)]
+    out = [pltpu.make_async_copy(held.at[h], hid.at[h], sems.at[8 + h]) for h in range(2)]
+    for cp in (loads[0], loads[1], xin[0], xin[1], loads[2]):
+        cp.start()
+    xin[0].wait()
+    for m in range(2):
+        loads[m].wait()
+        stores[m].start()
+    for h in range(2):
+        if h == 1:
+            xin[1].wait()
+            loads[2].wait()
+            stores[2].start()
+        held[h] = hidden_block(x[h], wv)[:, :units].reshape(held.shape[1:])
+        out[h].start()
+    for cp in stores + out:
+        cp.wait()
 
 
 def hidden_of(rows, ew):
-    count, units = 256, ew.shape[1]
+    units, width = ew.shape[1:]
+    padded = -(-units // 128) * 128
+    shape = (2,) + rows.shape[2:5] + (units,)
+    count = 2 * 16 * rows.shape[4]
+    hbm = pl.BlockSpec(memory_space=pltpu.HBM)
     return pl.pallas_call(
         hidden_kernel,
-        grid=(rows.shape[0] // count,),
-        out_shape=(
-            jax.ShapeDtypeStruct((rows.shape[0], units), BF16),
-            jax.ShapeDtypeStruct(ew.shape, BF16),
+        out_shape=(jax.ShapeDtypeStruct(shape, BF16), jax.ShapeDtypeStruct(ew.shape, BF16)),
+        in_specs=[hbm] * 2,
+        out_specs=[hbm] * 2,
+        scratch_shapes=[
+            pltpu.VMEM((2,) + rows.shape[2:], BF16),
+            pltpu.VMEM((2, padded, width), BF16),
+            pltpu.VMEM((units, width), BF16),
+            pltpu.VMEM(shape, BF16),
+            pltpu.SemaphoreType.DMA((10,)),
+        ],
+        compiler_params=pltpu.CompilerParams(vmem_limit_bytes=63 * 1024 * 1024),
+        cost_estimate=pl.CostEstimate(
+            flops=4 * count * units * width, bytes_accessed=4 * ew.size, transcendentals=count * units
         ),
-        in_specs=[
-            pl.BlockSpec((count, rows.shape[1]), lambda i: (i, 0)),
-            pl.BlockSpec(memory_space=pl.ANY),
-        ],
-        out_specs=[
-            pl.BlockSpec((count, units), lambda i: (i, 0)),
-            pl.BlockSpec(memory_space=pl.ANY),
-        ],
-        scratch_shapes=[
-            pltpu.VMEM((3, -(-units // 128) * 128, ew.shape[2]), BF16),
-            pltpu.SemaphoreType.DMA((6,)),
-        ],
-        compiler_params=pltpu.CompilerParams(vmem_limit_bytes=40 * 1024 * 1024),
     )(rows, ew)
 
 
 CHUNKS = (1, 3, 2, 0)
 
 
-def scatter_kernel(hid, ew, out, down, snd, r0, s0, r1, s1, r2, s2, r3, xs, xr, ss, rs, ls):
+def scatter_kernel(rows, hid_hbm, ew, out, x, wv, hid, down, snd, r0, s0, r1, s1, r2, s2, r3,
+                   xs, xr, ss, rs, ls):
     p = Place()
-    load = pltpu.make_async_copy(ew.at[2], down, ls)
-    load.start()
+    units = ew.shape[1]
+    parts = [(h, j) for j in CHUNKS[1:] for h in (1, 0)]
+
+    def fetch(n):
+        h, j = parts[n]
+        core = lax.rem(p.core + h, 2)
+        return pltpu.make_async_copy(rows.at[core, p.shift("z", j)], x.at[n % 2], ls.at[4 + n])
+
+    fetches = [fetch(n) for n in range(6)]
+    loads = [
+        pltpu.make_async_copy(ew.at[2], down, ls.at[0]),
+        pltpu.make_async_copy(hid_hbm, hid.at[:, p.shift("z", CHUNKS[0])], ls.at[1]),
+        pltpu.make_async_copy(ew.at[0], wv.at[0, pl.ds(0, units)], ls.at[2]),
+        pltpu.make_async_copy(ew.at[1], wv.at[1, pl.ds(0, units)], ls.at[3]),
+    ]
+    for cp in loads + fetches[:2]:
+        cp.start()
     bar = pltpu.get_barrier_semaphore()
     peers = [{"core": 1 - p.core}] + [p.along(a, k) for a in ("x", "y", "z") for k in (1, 2, 3)]
     for q in peers:
         pl.semaphore_signal(bar, inc=1, device_id=q, device_id_type=MESH)
     pl.semaphore_wait(bar, len(peers))
-    load.wait()
+    loads[0].wait()
+    loads[1].wait()
     cuts = colour_lanes(down.shape[1])
 
     def product(core, z, c):
@@ -377,11 +460,30 @@
                 cp.start()
             stage1[c] += copies
 
+    def compute(n):
+        h, j = parts[n]
+        fetches[n].wait()
+        value = hidden_block(x[n % 2], wv)[:, :units]
+        hid[lax.rem(p.core + h, 2), p.shift("z", j)] = value.reshape(hid.shape[2:])
+        if n + 2 < len(parts):
+            fetches[n + 2].start()
+
     give(CHUNKS[0])
-    for n in range(4):
-        if n < 3:
-            give(CHUNKS[n + 1])
-        take(CHUNKS[n])
+    loads[2].wait()
+    loads[3].wait()
+    compute(0)
+    give(CHUNKS[1])
+    take(CHUNKS[0])
+    compute(1)
+    compute(2)
+    take(CHUNKS[1])
+    give(CHUNKS[2])
+    compute(3)
+    compute(4)
+    give(CHUNKS[3])
+    take(CHUNKS[2])
+    compute(5)
+    take(CHUNKS[3])
 
     def pick(ref, left, axis, v):
         return ref.at[tuple(v if a == axis else slice(None) for a in left)]
@@ -439,9 +541,10 @@
         out[:, lo:lo + n] = total.astype(BF16)
 
 
-def scatter(hid, ew):
+def scatter(tall, hid, ew):
     rows, units = hid.shape[-2:]
     width = ew.shape[2]
+    padded = -(-units // 128) * 128
     cuts = colour_lanes(width)
     dma = pltpu.SemaphoreType.DMA
 
@@ -451,25 +554,26 @@
     return pl.pallas_call(
         scatter_kernel,
         out_shape=jax.ShapeDtypeStruct((rows, width), BF16),
-        in_specs=[pl.BlockSpec(memory_space=pltpu.VMEM), pl.BlockSpec(memory_space=pl.ANY)],
+        in_specs=[pl.BlockSpec(memory_space=pltpu.HBM)] * 3,
         out_specs=pl.BlockSpec(memory_space=pltpu.VMEM),
         scratch_shapes=[
+            pltpu.VMEM((2,) + tall.shape[2:], BF16),
+            pltpu.VMEM((2, padded, width), BF16),
+            pltpu.VMEM((2, 4, 4, 4, rows, units), BF16),
             pltpu.VMEM((units, width), BF16),
             bufs(4, 4, 4), bufs(4, 4, 4), bufs(4, 4, 4),
             bufs(3, 4, 4), bufs(4, 4), bufs(3, 4), bufs(4), bufs(3),
-            dma((12,)), dma((12,)), dma((60,)), dma((60,)), dma,
+            dma((12,)), dma((12,)), dma((60,)), dma((60,)), dma((10,)),
         ],
         compiler_params=pltpu.CompilerParams(
-            collective_id=1, has_side_effects=True, vmem_limit_bytes=56 * 1024 * 1024
+            collective_id=1, has_side_effects=True, vmem_limit_bytes=60 * 1024 * 1024
         ),
-    )(hid, ew)
+    )(tall, hid, ew)
 
 
 def local(attention_weights, ffn_weights, tokens, routes, router):
     experts = router.shape[1]
     width = tokens.shape[1]
-    wt = jnp.swapaxes(ffn_weights[0], 1, 2)
-    wt = wt.reshape(3, 4, 4, 2, wt.shape[1] // 32, wt.shape[2])
     gates = jax.nn.sigmoid(jnp.dot(tokens, router, preferred_element_type=F32))
     named = jnp.sum((routes[:, :, None] == jnp.arange(experts, dtype=jnp.int32)).astype(F32), axis=1)
     weighting = named * gates
@@ -479,11 +583,11 @@
     tok = jnp.concatenate(
         [tokens, high, low, jnp.zeros((tokens.shape[0], 128 - 2 * experts), BF16)], axis=1
     )
-    ew, tall, arecv = gather(wt, tok, attention_weights[0])
-    flat = tall.reshape(-1, tok.shape[1])
-    hid, kept = hidden_of(flat, ew)
-    mixed_output = scatter(hid.reshape(2, 4, 4, 4, tokens.shape[0], -1), kept)
-    merged = (jnp.sum(arecv.astype(F32), axis=0) * 0.25).astype(BF16)
+    ew, tall, near_sum, far_sum = gather(ffn_weights[0], tok, attention_weights[0])
+    hid, kept = hidden_of(tall, ew)
+    mixed_output = scatter(tall, hid, kept)
+    far = lax.ppermute(far_sum, "zl", [(0, 1), (1, 0)])
+    merged = ((near_sum + far.astype(F32)) * 0.25).astype(BF16)
     return merged, jnp.swapaxes(kept, 1, 2)[None], mixed_output
 
 

time: 263 us -> 227 us (0.86)
  Pallas kernels: 243 us -> 217 us
  local copies, waits for them, and re-layouts: 16 us -> 3.32 us
    pallas_call x1, Pallas kernels: 164 us -> 146 us  [gather(): pl.pallas_call(gather_kernel, out_shape=(jax.ShapeDtypeStruct((3, units,...]
    transpose x1 -> x0, local copies, waits for them, and re-layouts: 12.2 us -> none  [local(): wt = jnp.swapaxes(ffn_weights[0], 1, 2)]
    pallas_call x1, Pallas kernels: 18.7 us -> 8.82 us  [hidden_of(): pl.pallas_call(hidden_kernel, out_shape=(jax.ShapeDtypeStruct(shape, BF16...]
  transfers between devices with their start and end apart: 0 -> 1, of which waited for: 0 -> 0; matrix products, arithmetic and copies ran while one was open for 0% -> 0% of each run, Pallas kernels for 0% -> 32%
where the time goes in v3:
time: 227 us; the launch traced here: 224 us
  Pallas kernels  217 us (96%)
  local copies, waits for them, and re-layouts  3.32 us (1%)
    pallas_call x1, Pallas kernels, gather(): pl.pallas_call(gather_kernel, out_shape=(jax.ShapeDtypeStruct((3, units,...  146 us
    pallas_call x1, Pallas kernels, scatter(): pl.pallas_call(scatter_kernel, out_shape=jax.ShapeDtypeStruct((rows, widt...  62.7 us
    pallas_call x1, Pallas kernels, hidden_of(): pl.pallas_call(hidden_kernel, out_shape=(jax.ShapeDtypeStruct(shape, BF16...  8.82 us
  transfers between devices with their start and end apart: 1, of which 0 were waited for; matrix products, arithmetic and copies ran while one was open for 0% of the time, Pallas kernels for 32%

profile of v3, /device:TPU:0, one launch (start us, length us, event | category | flops | bytes accessed | tf_op | source)
XLA Modules:
  0.0 224.3 jit_solution(518466043664265189)
XLA Ops:
  0.6 0.0 copy-start
  0.6 0.7 convert_reduce_fusion
  1.3 0.1 copy.15
  1.4 0.0 copy-done
  1.4 1.1 fusion.4
  2.5 1.6 concatenate.3.tok
  4.2 145.8 %shard_map.76 = (bf16[3,344,4096]{2,1,0:T(8,128)(2,1)}, bf16[2,4,4,4,16,4224]{5,4,3,2,1,0:T(8,128)(2,1)}, f32[2,1024,128]{2,1,0:T(8,128)}, bf16[2,1024,128]{2,1,0:T(8,128)(2,1)}) custom-call(bf16[3,128,11008]{2,1,0:T(8,128)(2,1)} %bitcast.7, bf16[16,4224]{1,0:T(8,128)(2,1)} %concatenate.3.tok, bf16[2,4096,128]{2,1,0:T(8,128)(2,1)} %bitcast.9), custom_call_target="tpu_custom_call" | custom-call | tf_op jit(solution)/shard_map/pallas_call | solution.py:279
  150.0 0.3 collective-permute-start
  150.3 8.8 %shard_map.77 = (bf16[2,4,4,16,344]{4,3,2,1,0:T(8,128)(2,1)}, bf16[3,344,4096]{2,1,0:T(8,128)(2,1)}) custom-call(bf16[2,4,4,4,16,4224]{5,4,3,2,1,0:T(8,128)(2,1)} %get-tuple-element.11.rows, bf16[3,344,4096]{2,1,0:T(8,128)(2,1)} %get-tuple-element.12.ew), custom_call_target="tpu_custom_call" | custom-call | flops 2885681152 | bytes 16908288 | tf_op jit(solution)/shard_map/pallas_call | solution.py:361
  159.1 0.0 copy-start.1
  159.1 62.7 %shard_map.78 = bf16[16,4096]{1,0:T(8,128)(2,1)} custom-call(bf16[2,4,4,4,16,4224]{5,4,3,2,1,0:T(8,128)(2,1)} %get-tuple-element.11.rows, bf16[2,4,4,16,344]{4,3,2,1,0:T(8,128)(2,1)} %get-tuple-element.14.hid_hbm, bf16[3,344,4096]{2,1,0:T(8,128)(2,1)} %get-tuple-element.13.ew), custom_call_target="tpu_custom_call" | custom-call | tf_op jit(solution)/shard_map/pallas_call | solution.py:554
  221.8 0.0 collective-permute-done
  221.8 0.0 copy-done.1
  221.8 0.9 multiply_convert_fusion
  222.7 1.6 copy.18
  (1 shorter events, 0.0 us)
Async XLA Ops:
  0.6 0.8 copy-start
  150.0 71.8 %collective-permute-start = (bf16[2,1024,128]{2,1,0:T(8,128)(2,1)}, bf16[2,1024,128]{2,1,0:T(8,128)(2,1)S(1)}, u32[]{:S(2)}, u32[]{:S(2)}) collective-permute-start(bf16[2,1024,128]{2,1,0:T(8,128)(2,1)} %get-tuple-element.10), channel_id=1, source_target_pairs={{0,64},{64,0},{1,65},{65,1},{2,66},{66,2},{3,67},{67,3},{4,68},{68... | collective-permute-start | bytes 1572872 | tf_op jit(solution)/shard_map/ppermute | solution.py:589
  159.1 62.7 %copy-start.1 = (f32[2,1024,128]{2,1,0:T(8,128)S(1)}, f32[2,1024,128]{2,1,0:T(8,128)}, u32[]{:S(2)}) copy-start(f32[2,1024,128]{2,1,0:T(8,128)} %get-tuple-element.9) | copy-start | bytes 3145732

commit v4 on v3

--- a/solution.py
+++ b/solution.py
@@ -48,11 +48,12 @@
     return tuple(out)
 
 
-def gather_kernel(w, tok, att, ew, tall, near_sum, far_sum, raw, wt, b1, b2, turned, tbuf, aown, arecv,
+def gather_kernel(w, tok, ext, att, ew, tall, near_sum, far_sum, raw, wt, b1, b2, turned, tbuf, aown, arecv,
                   s1, r1, s2, r2, s3, r3, gs, gr, cs, cr, as_, ar, ls):
     p = Place()
     rows = att.shape[1] // 4
-    third = tok.shape[1] // 3
+    width = tok.shape[1]
+    third = tall.shape[-1] // 3
     units = ew.shape[1]
     pos = {"y": p.y, "x": p.x, "zh": p.zh}
 
@@ -64,9 +65,12 @@
             cp.start()
 
     loads = [pltpu.make_async_copy(w.at[m], raw.at[m], ls.at[m]) for m in range(3)]
-    tin = pltpu.make_async_copy(tok, tbuf, ls.at[3])
+    tins = [
+        pltpu.make_async_copy(tok, tbuf.at[:, pl.ds(0, width)], ls.at[3]),
+        pltpu.make_async_copy(ext, tbuf.at[:, pl.ds(width, ext.shape[1])], ls.at[47]),
+    ]
     tout = pltpu.make_async_copy(tbuf, tall.at[p.core, p.z, p.y, p.x], ls.at[4])
-    tin.start()
+    start(tins)
     start(loads)
     ours = [
         pltpu.make_async_copy(
@@ -89,16 +93,24 @@
     def gather_copies(phase, hops_):
         out = []
         for c, order in enumerate(ORDERS):
-            dst = tall.at[(p.core,) + block_index(p, order, phase) + (slice(None), lanes(c))]
-            src = tok.at[:, lanes(c)] if phase == 0 else dst
-            for k in hops_:
-                i = (phase * 3 + c) * 3 + k - 1
-                out.append(
-                    pltpu.make_async_remote_copy(
-                        src, dst, gs.at[i], gr.at[i],
-                        device_id=p.along(order[phase], k), device_id_type=MESH,
+            at = (p.core,) + block_index(p, order, phase) + (slice(None),)
+            dst = tall.at[at + (lanes(c),)]
+            pairs = [(dst, dst, (phase * 3 + c) * 3)]
+            if phase == 0:
+                end = min((c + 1) * third, width)
+                cut = pl.ds(c * third, end - c * third)
+                pairs = [(tok.at[:, cut], tall.at[at + (cut,)], c * 3)]
+                if c == 2:
+                    pairs.append((ext, tall.at[at + (pl.ds(width, ext.shape[1]),)], 33))
+            for src, dst, first in pairs:
+                for k in hops_:
+                    i = first + k - 1
+                    out.append(
+                        pltpu.make_async_remote_copy(
+                            src, dst, gs.at[i], gr.at[i],
+                            device_id=p.along(order[phase], k), device_id_type=MESH,
+                        )
                     )
-                )
         return out
 
     def relay_copies(back):
@@ -195,7 +207,8 @@
 
     start(phase0)
     start(acopies)
-    tin.wait()
+    for cp in tins:
+        cp.wait()
     tout.start()
     tout.wait()
 
@@ -270,21 +283,22 @@
         cp.wait()
 
 
-def gather(w, tok, att):
+def gather(w, tok, ext, att):
     units = w.shape[2] // 32
     depth = w.shape[1]
     rows = att.shape[1] // 4
     dma = pltpu.SemaphoreType.DMA
     split = (3, 4, 4, 2, units, depth)
+    wide = (tok.shape[0], tok.shape[1] + ext.shape[1])
     return pl.pallas_call(
         gather_kernel,
         out_shape=(
             jax.ShapeDtypeStruct((3, units, depth * 32), BF16),
-            jax.ShapeDtypeStruct((2, 4, 4, 4) + tok.shape, BF16),
+            jax.ShapeDtypeStruct((2, 4, 4, 4) + wide, BF16),
             jax.ShapeDtypeStruct((2, rows, att.shape[2]), F32),
             jax.ShapeDtypeStruct((2, rows, att.shape[2]), BF16),
         ),
-        in_specs=[pl.BlockSpec(memory_space=pl.ANY)] * 3,
+        in_specs=[pl.BlockSpec(memory_space=pltpu.HBM)] * 4,
         out_specs=[pl.BlockSpec(memory_space=pl.ANY)] * 2 + [pl.BlockSpec(memory_space=pltpu.VMEM)] * 2,
         scratch_shapes=[
             pltpu.VMEM(w.shape, BF16),
@@ -292,16 +306,16 @@
             pltpu.VMEM(split, BF16),
             pltpu.VMEM(split, BF16),
             pltpu.VMEM((w.shape[2], depth), F32),
-            pltpu.VMEM(tok.shape, BF16),
+            pltpu.VMEM(wide, BF16),
             pltpu.VMEM((2, 2, rows, att.shape[2]), BF16),
             pltpu.VMEM((2, 2, rows, att.shape[2]), BF16),
             dma((9,)), dma((9,)), dma((24,)), dma((24,)), dma((64,)), dma((64,)),
-            dma((33,)), dma((33,)), dma((12,)), dma((12,)), dma((2,)), dma((2,)), dma((48,)),
+            dma((36,)), dma((36,)), dma((12,)), dma((12,)), dma((2,)), dma((2,)), dma((48,)),
         ],
         compiler_params=pltpu.CompilerParams(
             collective_id=0, has_side_effects=True, vmem_limit_bytes=56 * 1024 * 1024
         ),
-    )(w, tok, att)
+    )(w, tok, ext, att)
 
 
 def colour_lanes(width):
@@ -377,10 +391,10 @@
     )(rows, ew)
 
 
-CHUNKS = (1, 3, 2, 0)
-
-
-def scatter_kernel(rows, hid_hbm, ew, out, x, wv, hid, down, snd, r0, s0, r1, s1, r2, s2, r3,
+CHUNKS = (2, 1, 3, 0)
+
+
+def scatter_kernel(rows, hid_hbm, ew, out, x, wv, hid, down, snd, r0, s0, e1, r1, s1, r2, s2, r3,
                    xs, xr, ss, rs, ls):
     p = Place()
     units = ew.shape[1]
@@ -398,8 +412,8 @@
         pltpu.make_async_copy(ew.at[0], wv.at[0, pl.ds(0, units)], ls.at[2]),
         pltpu.make_async_copy(ew.at[1], wv.at[1, pl.ds(0, units)], ls.at[3]),
     ]
-    for cp in loads + fetches[:2]:
-        cp.start()
+    loads[0].start()
+    loads[1].start()
     bar = pltpu.get_barrier_semaphore()
     peers = [{"core": 1 - p.core}] + [p.along(a, k) for a in ("x", "y", "z") for k in (1, 2, 3)]
     for q in peers:
@@ -407,6 +421,8 @@
     pl.semaphore_wait(bar, len(peers))
     loads[0].wait()
     loads[1].wait()
+    for cp in loads[2:] + fetches[:2]:
+        cp.start()
     cuts = colour_lanes(down.shape[1])
 
     def product(core, z, c):
@@ -423,7 +439,7 @@
         )
 
     swaps = {(j, c): swap(j, c) for j in range(4) for c in range(3)}
-    number = iter(range(60))
+    number = iter(range(63))
 
     def remote(src, dst, axis, k):
         i = next(number)
@@ -437,7 +453,16 @@
             snd[c][z] = product(1 - p.core, z, c).astype(BF16)
             swaps[j, c].start()
 
-    stage1 = [[], [], []]
+    early, stage1 = {}, {}
+    halves = (pl.ds(0, 2), pl.ds(2, 2))
+
+    def begin(copies):
+        for cp in copies:
+            cp.start()
+        return copies
+
+    def slab(c, z, v, part=slice(None)):
+        return s0[c].at[z, part, v] if c == 0 else s0[c].at[z, v, part]
 
     def take(j):
         z = p.shift("z", j)
@@ -446,19 +471,45 @@
             swaps[j, c].wait()
             s0[c][z] = (value + r0[c][z].astype(F32)).astype(BF16)
             axis = order[0]
-            if axis == "z":
-                copies = [remote(s0[c].at[z], r1[c].at[j - 1], "z", j)] if j else []
-            elif axis == "y":
-                copies = [
-                    remote(s0[c].at[z, p.shift("y", k)], r1[c].at[k - 1, z], "y", k) for k in (1, 3, 2)
-                ]
-            else:
-                copies = [
-                    remote(s0[c].at[z, :, p.shift("x", k)], r1[c].at[k - 1, z], "x", k) for k in (1, 3, 2)
-                ]
-            for cp in copies:
-                cp.start()
-            stage1[c] += copies
+            if axis != "z":
+                far = p.shift(axis, 2)
+                early[c, j] = begin([
+                    remote(slab(c, z, far, halves[i]), e1[c].at[i, z], axis, k) for i, k in ((0, 1), (1, 3))
+                ])
+            elif j == 2:
+                early[c] = begin([
+                    remote(s0[c].at[z, halves[i]], e1[c].at[i], axis, k) for i, k in ((0, 1), (1, 3))
+                ])
+            elif j:
+                i = 0 if j == 1 else 1
+                early[c][i].wait()
+
+                def join(n, carry, c=c, i=i):
+                    at = (z, i * 2 + n // 4, lax.rem(n, 4))
+                    term = e1[c][i, n // 4, lax.rem(n, 4)].astype(F32)
+                    s0[c][at] = (s0[c][at].astype(F32) + term).astype(BF16)
+                    return carry
+
+                lax.fori_loop(0, 8, join, 0)
+                stage1[c, j] = begin([remote(s0[c].at[z], r1[c].at[i], axis, j)])
+
+    def relay(j):
+        z = p.shift("z", j)
+        for c in (0, 1):
+            axis = ORDERS[c][0]
+            for cp in early[c, j]:
+                cp.wait()
+            stage1[c, j] = []
+            for i, k in ((0, 1), (1, 3)):
+                v = p.shift(axis, k)
+
+                def join(n, carry, c=c, i=i, v=v):
+                    at = (z, i * 2 + n, v) if c == 0 else (z, v, i * 2 + n)
+                    s0[c][at] = (s0[c][at].astype(F32) + e1[c][i, z, n].astype(F32)).astype(BF16)
+                    return carry
+
+                lax.fori_loop(0, 2, join, 0)
+                stage1[c, j] += begin([remote(slab(c, z, v), r1[c].at[i, z], axis, k)])
 
     def compute(n):
         h, j = parts[n]
@@ -468,22 +519,56 @@
         if n + 2 < len(parts):
             fetches[n + 2].start()
 
-    give(CHUNKS[0])
+    stage2, stage3 = {}, []
+
+    def reduce(j):
+        z = p.shift("z", j)
+        for c in (0, 1):
+            for cp in stage1[c, j]:
+                cp.wait()
+
+            def add(i, carry, c=c):
+                mine = s0[c][z, i, p.x] if c == 0 else s0[c][z, p.y, i]
+                total = mine.astype(F32)
+                for k in range(2):
+                    total += r1[c][k, z, i].astype(F32)
+                s1[c][z, i] = total.astype(BF16)
+                return carry
+
+            lax.fori_loop(0, 4, add, 0)
+            if c == 0:
+                copies = [
+                    remote(s1[c].at[z, p.shift("y", k)], r2[c].at[k - 1, z], "y", k) for k in (1, 3, 2)
+                ]
+            else:
+                copies = [remote(s1[c].at[z], r2[c].at[j - 1], "z", j)] if j else []
+            for cp in copies:
+                cp.start()
+            stage2[c] = stage2.get(c, []) + copies
+
+    give(2)
     loads[2].wait()
     loads[3].wait()
     compute(0)
-    give(CHUNKS[1])
-    take(CHUNKS[0])
+    give(1)
+    take(2)
     compute(1)
     compute(2)
-    take(CHUNKS[1])
-    give(CHUNKS[2])
+    take(1)
+    relay(2)
+    give(3)
     compute(3)
+    relay(1)
+    take(3)
     compute(4)
-    give(CHUNKS[3])
-    take(CHUNKS[2])
+    give(0)
+    relay(3)
+    reduce(2)
     compute(5)
-    take(CHUNKS[3])
+    take(0)
+    reduce(1)
+    relay(0)
+    reduce(3)
 
     def pick(ref, left, axis, v):
         return ref.at[tuple(v if a == axis else slice(None) for a in left)]
@@ -497,23 +582,21 @@
             cp.start()
         return copies
 
-    stage2, stage3 = [], []
-    for c, order in enumerate(ORDERS):
-        for cp in stage1[c]:
-            cp.wait()
-        mine = pick(s0[c], left_after(order, 0), order[0], p.at[order[0]])
-
-        def add(i, carry, c=c, mine=mine):
-            at = (i // 4, lax.rem(i, 4))
-            total = mine[at].astype(F32)
-            for k in range(3):
-                total += r1[c][(k,) + at].astype(F32)
-            s1[c][at] = total.astype(BF16)
-            return carry
-
-        lax.fori_loop(0, 16, add, 0)
-        left = left_after(order, 1)
-        stage2.append(send(c, order[1], lambda v, c=c, left=left, a=order[1]: pick(s1[c], left, a, v), r2[c]))
+    for j in (1, 3):
+        stage1[2, j][0].wait()
+    own = p.z
+
+    def add(i, carry):
+        at = (i // 4, lax.rem(i, 4))
+        total = s0[2][(own,) + at].astype(F32)
+        for k in range(2):
+            total += r1[2][(k,) + at].astype(F32)
+        s1[2][at] = total.astype(BF16)
+        return carry
+
+    lax.fori_loop(0, 16, add, 0)
+    stage2[2] = send(2, "x", lambda v: s1[2].at[:, v], r2[2])
+    reduce(0)
 
     for c, order in enumerate(ORDERS):
         for cp in stage2[c]:
@@ -562,8 +645,10 @@
             pltpu.VMEM((2, 4, 4, 4, rows, units), BF16),
             pltpu.VMEM((units, width), BF16),
             bufs(4, 4, 4), bufs(4, 4, 4), bufs(4, 4, 4),
-            bufs(3, 4, 4), bufs(4, 4), bufs(3, 4), bufs(4), bufs(3),
-            dma((12,)), dma((12,)), dma((60,)), dma((60,)), dma((10,)),
+            [pltpu.VMEM(lead + (rows, n), BF16)
+             for lead, (_, n) in zip(((2, 4, 2), (2, 4, 2), (2, 2, 4)), cuts)],
+            bufs(2, 4, 4), bufs(4, 4), bufs(3, 4), bufs(4), bufs(3),
+            dma((12,)), dma((12,)), dma((63,)), dma((63,)), dma((10,)),
         ],
         compiler_params=pltpu.CompilerParams(
             collective_id=1, has_side_effects=True, vmem_limit_bytes=60 * 1024 * 1024
@@ -580,10 +665,10 @@
     high = lax.reduce_precision(weighting, 8, 7)
     low = (weighting - high).astype(BF16)
     high = high.astype(BF16)
-    tok = jnp.concatenate(
-        [tokens, high, low, jnp.zeros((tokens.shape[0], 128 - 2 * experts), BF16)], axis=1
+    ext = jnp.concatenate(
+        [high, low, jnp.zeros((tokens.shape[0], 128 - 2 * experts), BF16)], axis=1
     )
-    ew, tall, near_sum, far_sum = gather(ffn_weights[0], tok, attention_weights[0])
+    ew, tall, near_sum, far_sum = gather(ffn_weights[0], tokens, ext, attention_weights[0])
     hid, kept = hidden_of(tall, ew)
     mixed_output = scatter(tall, hid, kept)
     far = lax.ppermute(far_sum, "zl", [(0, 1), (1, 0)])

time: 227 us -> 225 us (level)
  no operation moved by 1% of the time
where the time goes in v4:
time: 225 us; the launch traced here: 224 us
  Pallas kernels  218 us (97%)
  other arithmetic  2.31 us (1%)
    pallas_call x1, Pallas kernels, gather(): pl.pallas_call(gather_kernel, out_shape=(jax.ShapeDtypeStruct((3, units,...  146 us
    pallas_call x1, Pallas kernels, scatter(): pl.pallas_call(scatter_kernel, out_shape=jax.ShapeDtypeStruct((rows, widt...  63.6 us
    pallas_call x1, Pallas kernels, hidden_of(): pl.pallas_call(hidden_kernel, out_shape=(jax.ShapeDtypeStruct(shape, BF16...  8.82 us
  transfers between devices with their start and end apart: 1, of which 0 were waited for; matrix products, arithmetic and copies ran while one was open for 0% of the time, Pallas kernels for 32%

profile of v4, /device:TPU:0, one launch (start us, length us, event | category | flops | bytes accessed | tf_op | source)
XLA Modules:
  0.0 224.4 jit_solution(189202701818346730)
XLA Ops:
  0.6 0.0 copy-start
  0.6 0.7 convert_reduce_fusion
  1.3 0.1 copy.15
  1.4 0.1 pad.2.clone
  1.5 0.0 copy-done
  1.5 1.1 reduce-precision_convert_fusion
  2.6 0.7 maximum_maximum_fusion.ext
  3.3 145.9 %shard_map.76 = (bf16[3,344,4096]{2,1,0:T(8,128)(2,1)}, bf16[2,4,4,4,16,4224]{5,4,3,2,1,0:T(8,128)(2,1)}, f32[2,1024,128]{2,1,0:T(8,128)}, bf16[2,1024,128]{2,1,0:T(8,128)(2,1)}) custom-call(bf16[3,128,11008]{2,1,0:T(8,128)(2,1)} %bitcast.7, bf16[16,4096]{1,0:T(8,128)(2,1)} %tok.1, bf16[16,128]{1,0:T(8,128)(2,1)} %maximum_maximum_fusion.ext, ...), custom_call_target="tpu_custom_call" | custom-call | tf_op jit(solution)/shard_map/pallas_call | solution.py:293
  149.2 0.3 collective-permute-start
  149.4 8.8 %shard_map.77 = (bf16[2,4,4,16,344]{4,3,2,1,0:T(8,128)(2,1)}, bf16[3,344,4096]{2,1,0:T(8,128)(2,1)}) custom-call(bf16[2,4,4,4,16,4224]{5,4,3,2,1,0:T(8,128)(2,1)} %get-tuple-element.11.rows, bf16[3,344,4096]{2,1,0:T(8,128)(2,1)} %get-tuple-element.12.ew), custom_call_target="tpu_custom_call" | custom-call | flops 2885681152 | bytes 16908288 | tf_op jit(solution)/shard_map/pallas_call | solution.py:375
  158.3 0.0 copy-start.1
  158.3 63.6 %shard_map.78 = bf16[16,4096]{1,0:T(8,128)(2,1)} custom-call(bf16[2,4,4,4,16,4224]{5,4,3,2,1,0:T(8,128)(2,1)} %get-tuple-element.11.rows, bf16[2,4,4,16,344]{4,3,2,1,0:T(8,128)(2,1)} %get-tuple-element.14.hid_hbm, bf16[3,344,4096]{2,1,0:T(8,128)(2,1)} %get-tuple-element.13.ew), custom_call_target="tpu_custom_call" | custom-call | tf_op jit(solution)/shard_map/pallas_call | solution.py:637
  221.8 0.0 collective-permute-done
  221.9 0.0 copy-done.1
  221.9 0.9 multiply_convert_fusion
  222.8 1.6 copy.18
  (1 shorter events, 0.0 us)
Async XLA Ops:
  0.6 0.9 copy-start
  149.2 72.7 %collective-permute-start = (bf16[2,1024,128]{2,1,0:T(8,128)(2,1)}, bf16[2,1024,128]{2,1,0:T(8,128)(2,1)S(1)}, u32[]{:S(2)}, u32[]{:S(2)}) collective-permute-start(bf16[2,1024,128]{2,1,0:T(8,128)(2,1)} %get-tuple-element.10), channel_id=1, source_target_pairs={{0,64},{64,0},{1,65},{65,1},{2,66},{66,2},{3,67},{67,3},{4,68},{68... | collective-permute-start | bytes 1572872 | tf_op jit(solution)/shard_map/ppermute | solution.py:674
  158.3 63.6 %copy-start.1 = (f32[2,1024,128]{2,1,0:T(8,128)S(1)}, f32[2,1024,128]{2,1,0:T(8,128)}, u32[]{:S(2)}) copy-start(f32[2,1024,128]{2,1,0:T(8,128)} %get-tuple-element.9) | copy-start | bytes 3145732
